TPU v7x, 32 devices: a whole 2x2x4 slice. The times are simulated.
32 devices in a mesh: layer: 4 (over z), facet: 8 (over y, x, core).
Axes of the slice: x: 2, y: 2, z: 4, core: 2. Of those that a mesh axis runs over, the one named last changes fastest.
Arguments:
- model_strip: bfloat16 [8, 2, 64, 8192], P('facet', None, None, 'layer'), may hold values from -6 to 6
- screen_angle: bfloat16 [4, 8, 64, 8192], P('layer', 'facet'), may hold values from -3.140625 to 3.140625
- facet_window: float32 [8, 8192], P('facet'), may hold values from 0.04 to 0.16
- facet_shift: int32 [8], P('facet'), may hold values from 0 to 8191
- kernel_taps: float32 [7], replicated, may hold values from 0.2 to 0.6
- plane_angle: float32 [4, 8], P('layer'), may hold values from -3.140625 to 3.140625
- u_cell: int32 [4, 128, 512], P('layer', 'facet'), may hold values from 0 to 63
- v_cell: int32 [4, 128, 512], P('layer', 'facet'), may hold values from 0 to 63
- w_plane: int32 [4, 128, 512], P('layer', 'facet'), may hold values from 0 to 7
- observed: float32 [4, 128, 2, 512], P('layer', 'facet'), may hold values from -6 to 6
Outputs:
- residual: float32 [4, 128, 2, 512], P('layer', 'facet')
- gradient: float32 [8, 2, 64, 8192], P('facet', None, None, 'layer')
All inputs are finite; a program needn't handle non-finite values.
Results may differ from a plain program's by a relative error of at most 0.009.
Values may be sent and summed in bfloat16 or wider, within the bound.
A program may use at most 64 MiB of HBM per device.

v0:
```python
import functools
import math

import jax
import jax.numpy as jnp
import numpy as np
from jax import lax
from jax.experimental import pallas as pl
from jax.experimental.pallas import tpu as pltpu
from jax.sharding import PartitionSpec as P

MESH = pl.DeviceIdType.MESH
BACK_GAIN = 8.0
CHUNKS = 8


def _fit(values, degree):
    nodes = np.cos(np.pi * (np.arange(64) + 0.5) / 64)
    y = (nodes + 1.0) * 0.5 * np.pi**2
    cheb = np.polynomial.chebyshev.Chebyshev.fit(y, values(np.sqrt(y)), degree, domain=[0, np.pi**2])
    return [float(v) for v in cheb.convert(kind=np.polynomial.Polynomial).coef]


COS = _fit(np.cos, 8)
SIN = _fit(lambda x: np.sinc(x / np.pi), 7)


def cos_sin(x):
    y = x * x
    c = jnp.full_like(y, COS[-1])
    for v in COS[-2::-1]:
        c = c * y + v
    s = jnp.full_like(y, SIN[-1])
    for v in SIN[-2::-1]:
        s = s * y + v
    return c, s * x


def dft(length):
    k = np.arange(length)
    angles = 2.0 * np.pi * ((k[:, None] * k[None, :]) % length) / length
    scale = 1.0 / math.sqrt(length)
    return np.cos(angles) * scale, -np.sin(angles) * scale


def barrier_line(i, n):
    sem = pltpu.get_barrier_semaphore()

    @pl.when(i > 0)
    def _():
        pl.semaphore_signal(sem, inc=1, device_id={"layer": i - 1}, device_id_type=MESH)

    @pl.when(i < n - 1)
    def _():
        pl.semaphore_signal(sem, inc=1, device_id={"layer": i + 1}, device_id_type=MESH)

    peers = jnp.where(i > 0, 1, 0) + jnp.where(i < n - 1, 1, 0)
    pl.semaphore_wait(sem, peers)


def forward_kernel(n, x_ref, ang_ref, f1_ref, g_ref, tw_ref, fac_ref, out_ref, buf, send_sem, recv_sem, own_sem):
    i = lax.axis_index("layer")
    cq = x_ref.shape[0] // CHUNKS
    subgrids = g_ref.shape[0] // 2
    rows = f1_ref.shape[0] // 2
    barrier_line(i, n)
    own = pltpu.make_async_copy(x_ref, buf.at[i], own_sem)
    own.start()

    def copy(direction, s, q):
        step = 1 if direction == 0 else -1
        origin = jnp.clip(i - step * s, 0, n - 1)
        cols = pl.ds(q * cq, cq)
        src = x_ref.at[cols] if s == 0 else buf.at[origin, cols]
        return pltpu.make_async_remote_copy(
            src_ref=src,
            dst_ref=buf.at[origin, cols],
            send_sem=send_sem.at[direction, s, q],
            recv_sem=recv_sem.at[direction, s, q],
            device_id={"layer": jnp.clip(i + step, 0, n - 1)},
            device_id_type=MESH,
        )

    def sends(direction, s):
        if direction == 0:
            return (i - s >= 0) & (i < n - 1)
        return (i + s <= n - 1) & (i > 0)

    def gets(direction, s):
        return i - 1 - s >= 0 if direction == 0 else i + 1 + s <= n - 1

    def compute(q):
        twr, twi = tw_ref[0], tw_ref[1]
        facr, faci = fac_ref[0], fac_ref[1]
        for pair in range(cq // 2):
            halves = []
            for c in (2 * pair, 2 * pair + 1):
                col = q * cq + c
                xr = jnp.concatenate([buf[l, col, 0] for l in range(n)], axis=0).astype(jnp.float32)
                xi = jnp.concatenate([buf[l, col, 1] for l in range(n)], axis=0).astype(jnp.float32)
                cosine, sine = cos_sin(ang_ref[col].astype(jnp.float32))
                x = jnp.concatenate([xr * cosine - xi * sine, xr * sine + xi * cosine], axis=0)
                h = jnp.dot(f1_ref[...], x.astype(jnp.bfloat16), preferred_element_type=jnp.float32)
                hr, hi = h[:rows], h[rows:]
                halves.append(
                    jnp.concatenate([hr * twr - hi * twi, hr * twi + hi * twr], axis=1).astype(jnp.bfloat16)
                )
            both = jnp.concatenate(halves, axis=0)
            spec = lax.dot_general(
                g_ref[...], both, (((1,), (1,)), ((), ())), preferred_element_type=jnp.float32
            )
            sr, si = spec[:subgrids], spec[subgrids:]
            at = q * (cq // 2) + pair
            out_ref[0, at] = (sr * facr - si * faci).astype(jnp.bfloat16)
            out_ref[1, at] = (sr * faci + si * facr).astype(jnp.bfloat16)

    def body(t, carry):
        @pl.when(t < CHUNKS)
        def _():
            for d in range(2):
                @pl.when(sends(d, 0))
                def _():
                    copy(d, 0, t).start()

        for s in range(n - 1):
            q = t - 1 - s
            @pl.when((q >= 0) & (q < CHUNKS))
            def _():
                for d in range(2):
                    @pl.when(gets(d, s))
                    def _():
                        copy(d, s, q).wait_recv()
                        if s + 1 < n - 1:
                            @pl.when(sends(d, s + 1))
                            def _():
                                copy(d, s + 1, q).start()

        @pl.when(t >= n - 1)
        def _():
            compute(t - (n - 1))

        return carry

    own.wait()
    lax.fori_loop(0, CHUNKS + n - 1, body, 0)

    def drain(q, carry):
        for d in range(2):
            for s in range(n - 1):
                @pl.when(sends(d, s))
                def _():
                    copy(d, s, q).wait_send()
        return carry

    lax.fori_loop(0, CHUNKS, drain, 0)


def backward_kernel(n, a_ref, ang_ref, g_ref, f2_ref, tw_ref, fac_ref, out_ref, term, sbuf, rbuf, send_sem, recv_sem):
    i = lax.axis_index("layer")
    cols = ang_ref.shape[0]
    cq = cols // CHUNKS
    fine = g_ref.shape[0] // 2
    rows = ang_ref.shape[1]
    part = rows // n
    barrier_line(i, n)

    def copy(direction, j, q):
        where = pl.ds(q * cq, cq)
        step = 1 if direction == 0 else -1
        return pltpu.make_async_remote_copy(
            src_ref=sbuf.at[direction, j, where],
            dst_ref=rbuf.at[direction, j, where],
            send_sem=send_sem.at[direction, j, q],
            recv_sem=recv_sem.at[direction, j, q],
            device_id={"layer": jnp.clip(i + step, 0, n - 1)},
            device_id_type=MESH,
        )

    def behind(direction):
        return i > 0 if direction == 0 else i < n - 1

    def compute(q):
        twr, twi = tw_ref[0], tw_ref[1]
        facr, faci = fac_ref[0], fac_ref[1]
        for pair in range(cq // 2):
            at = q * (cq // 2) + pair
            ar = a_ref[0, at].astype(jnp.float32)
            ai = a_ref[1, at].astype(jnp.float32)
            b = jnp.concatenate([ar * facr + ai * faci, ai * facr - ar * faci], axis=0).astype(jnp.bfloat16)
            h = jnp.dot(g_ref[...], b, preferred_element_type=jnp.float32)
            hr, hi = h[:fine], h[fine:]
            mixed = jnp.concatenate([hr * twr + hi * twi, hi * twr - hr * twi], axis=1).astype(jnp.bfloat16)
            image = lax.dot_general(
                f2_ref[...], mixed, (((1,), (1,)), ((), ())), preferred_element_type=jnp.float32
            )
            for c in range(2):
                col = q * cq + 2 * pair + c
                ir = image[2 * c * rows : (2 * c + 1) * rows]
                ii = image[(2 * c + 1) * rows : (2 * c + 2) * rows]
                cosine, sine = cos_sin(ang_ref[col].astype(jnp.float32))
                tr = (BACK_GAIN * (ir * cosine + ii * sine)).astype(jnp.bfloat16)
                ti = (BACK_GAIN * (ii * cosine - ir * sine)).astype(jnp.bfloat16)
                for l in range(n):
                    term[l, col, 0] = tr[l * part : (l + 1) * part]
                    term[l, col, 1] = ti[l * part : (l + 1) * part]

    def relay(direction, j, q):
        where = pl.ds(q * cq, cq)

        @pl.when(behind(direction))
        def _():
            copy(direction, j, q).wait_recv()
            total = term[j, where].astype(jnp.float32) + rbuf[direction, j, where].astype(jnp.float32)
            sbuf[direction, j, where] = total.astype(jnp.bfloat16)

        @pl.when(jnp.logical_not(behind(direction)))
        def _():
            sbuf[direction, j, where] = term[j, where]

        copy(direction, j, q).start()

    def body(t, carry):
        @pl.when(t < CHUNKS)
        def _():
            compute(t)

        for direction in range(2):
            q = t - i if direction == 0 else t - (n - 1 - i)

            @pl.when((q >= 0) & (q < CHUNKS))
            def _():
                for d in range(n - 1, 0, -1):
                    j = i + d if direction == 0 else i - d

                    @pl.when((j < n) & (j >= 0))
                    def _():
                        relay(direction, j, q)

        last = t - (n - 1)

        @pl.when(last >= 0)
        def _():
            where = pl.ds(last * cq, cq)
            out_ref[where] = term[i, where].astype(jnp.float32)
            for direction in range(2):
                @pl.when(behind(direction))
                def _():
                    copy(direction, i, last).wait_recv()
                    out_ref[where] += rbuf[direction, i, where].astype(jnp.float32)

        return carry

    lax.fori_loop(0, CHUNKS + n - 1, body, 0)

    def drain(q, carry):
        for direction in range(2):
            for d in range(1, n):
                j = i + d if direction == 0 else i - d

                @pl.when((j < n) & (j >= 0))
                def _():
                    copy(direction, j, q).wait_send()
        return carry

    lax.fori_loop(0, CHUNKS, drain, 0)


def facet_factor(window, shift_cells, subgrids):
    length = window.shape[0]
    rows = length // subgrids
    grid = window.reshape(subgrids, rows)
    grid = jnp.concatenate([grid, grid], axis=1)
    high = lax.broadcasted_iota(jnp.int32, grid.shape, 0)
    low = lax.broadcasted_iota(jnp.int32, grid.shape, 1) % rows
    turn_count = (high * rows + low) * shift_cells % length
    angles = 2.0 * math.pi / length * turn_count.astype(jnp.float32)
    return jnp.stack([grid * jnp.cos(angles), -grid * jnp.sin(angles)])


def spread(cells, length, taps):
    count = taps.shape[0]
    lanes = jnp.arange(length, dtype=jnp.int32)
    offset = (lanes - cells[..., None] + (count // 2 + length)) % length
    out = jnp.zeros(offset.shape, jnp.float32)
    for t in range(count):
        out = out + jnp.where(offset == t, taps[t], 0.0)
    return out


def middle(grids, u, v, plane, observed, angle, taps, rows, cols):
    row_weights = spread(u, rows, taps)
    column_weights = spread(v, cols, taps).astype(jnp.bfloat16)
    picked = jnp.einsum("sjc,sck->sjk", column_weights, grids.astype(jnp.bfloat16), preferred_element_type=jnp.float32)
    model_real = jnp.sum(picked[..., :rows] * row_weights, axis=2)
    model_imag = jnp.sum(picked[..., rows:] * row_weights, axis=2)
    pick = plane[..., None] == jnp.arange(angle.shape[0], dtype=jnp.int32)
    cosine = jnp.sum(jnp.where(pick, jnp.cos(angle), 0.0), axis=2)
    sine = jnp.sum(jnp.where(pick, jnp.sin(angle), 0.0), axis=2)
    res_real = observed[:, 0] - (model_real * cosine - model_imag * sine)
    res_imag = observed[:, 1] - (model_real * sine + model_imag * cosine)
    w_real = res_real * cosine + res_imag * sine
    w_imag = res_imag * cosine - res_real * sine
    spread_rows = jnp.concatenate(
        [w_real[..., None] * row_weights, w_imag[..., None] * row_weights], axis=2
    ).astype(jnp.bfloat16)
    adjoint = jnp.einsum("sjc,sjk->sck", column_weights, spread_rows, preferred_element_type=jnp.float32)
    return jnp.stack([res_real, res_imag], axis=1), adjoint.astype(jnp.bfloat16)


def middle_kernel(
    contrib_ref, u_ref, v_ref, plane_ref, obs_ref, taps_ref, table_ref, res_ref, out_ref,
    r0, acc0, r1, acc1, r2, fin, adj, phase, row_table, column_table, s0, d0, s1, d1, s2, d2, sg, dg,
):
    pairs = contrib_ref.shape[1]
    per, vis = u_ref.shape
    rows = contrib_ref.shape[3] // 2
    cols = 2 * pairs
    f = lax.axis_index("facet")
    core = lax.rem(f, 2)
    chip = lax.div(f, 2)
    bits = (lax.rem(chip, 2), lax.div(chip, 2))

    def flip(b):
        return f + (1 - 2 * bits[b]) * (2 * (1 + b))

    other = f + 1 - 2 * core
    barrier = pltpu.get_barrier_semaphore()
    for peer in (other, flip(0), flip(1)):
        pl.semaphore_signal(barrier, inc=1, device_id={"facet": peer}, device_id_type=MESH)
    pl.semaphore_wait(barrier, 3)

    def rows_of(device):
        return pl.ds(pl.multiple_of(device * per, per), per)

    def compose(p, along, across):
        return along + 2 * across if p == 0 else across + 2 * along

    def remote(src, dst, send, recv, device):
        return pltpu.make_async_remote_copy(
            src_ref=src, dst_ref=dst, send_sem=send, recv_sem=recv,
            device_id={"facet": device}, device_id_type=MESH,
        )

    def stage0(p, h):
        return remote(
            contrib_ref.at[p, :, rows_of(2 * h + 1 - core)], r0.at[p, h], s0.at[p, h], d0.at[p, h], other
        )

    def stage1(p, k):
        return remote(acc0.at[p, compose(p, 1 - bits[p], k)], r1.at[p, k], s1.at[p, k], d1.at[p, k], flip(p))

    def stage2(p):
        return remote(acc1.at[p, 1 - bits[1 - p]], r2.at[p], s2.at[p], d2.at[p], flip(1 - p))

    def add0(p, h):
        stage0(p, h).wait_recv()
        mine = contrib_ref[p, :, rows_of(2 * h + core)].astype(jnp.float32)
        acc0[p, h] = (mine + r0[p, h].astype(jnp.float32)).astype(jnp.bfloat16)

    order = [(a, k, p) for a in (1, 0) for k in range(2) for p in range(2)]
    for a, k, p in order:
        stage0(p, compose(p, 1 - bits[p] if a else bits[p], k)).start()
    for k in range(2):
        for p in range(2):
            add0(p, compose(p, 1 - bits[p], k))
            stage1(p, k).start()
    for k in range(2):
        for p in range(2):
            add0(p, compose(p, bits[p], k))

    plane = plane_ref[...]
    cosine = jnp.zeros(plane.shape, jnp.float32)
    sine = jnp.zeros(plane.shape, jnp.float32)
    for k in range(table_ref.shape[1]):
        hit = plane == k
        cosine = jnp.where(hit, table_ref[0, k], cosine)
        sine = jnp.where(hit, table_ref[1, k], sine)
    phase[0] = cosine
    phase[1] = sine

    def weights(cells, position, length):
        count = taps_ref.shape[0]
        offset = position - cells + count // 2
        offset = jnp.where(offset < 0, offset + length, jnp.where(offset >= length, offset - length, offset))
        out = jnp.zeros(offset.shape, jnp.float32)
        for t in range(count):
            out = jnp.where(offset == t, taps_ref[t], out)
        return out

    def prepare(s, carry):
        at = pl.ds(s, 1)
        row = lax.broadcasted_iota(jnp.int32, (rows, vis), 0)
        half = lax.broadcasted_iota(jnp.int32, (pairs, vis), 0)
        col = jnp.concatenate([2 * half, 2 * half + 1], axis=0)
        row_table[s] = weights(u_ref[at, :], row, rows)
        column_table[s] = weights(v_ref[at, :], col, cols).astype(jnp.bfloat16)
        return carry

    lax.fori_loop(0, per, prepare, 0)

    for k in range(2):
        for p in range(2):
            stage1(p, k).wait_recv()
            total = acc0[p, compose(p, bits[p], k)].astype(jnp.float32) + r1[p, k].astype(jnp.float32)
            acc1[p, k] = total.astype(jnp.bfloat16)
    for p in range(2):
        stage2(p).start()
    for p in range(2):
        stage2(p).wait_recv()
        for t in range(pairs):
            total = acc1[p, bits[1 - p], t].astype(jnp.float32) + r2[p, t].astype(jnp.float32)
            fin[p, pl.ds(t, per, stride=pairs), :] = total

    def one(s):
        at = pl.ds(s, 1)
        where = pl.ds(pl.multiple_of(s * pairs, pairs), pairs)
        row_weights = row_table[s]
        column_weights = column_table[s]
        real, imag = fin[0, where, :], fin[1, where, :]
        grid = jnp.concatenate(
            [
                jnp.concatenate([real[:, :rows], imag[:, :rows]], axis=1),
                jnp.concatenate([real[:, rows:], imag[:, rows:]], axis=1),
            ],
            axis=0,
        )
        picked = lax.dot_general(
            grid.astype(jnp.bfloat16), column_weights, (((0,), (0,)), ((), ())),
            preferred_element_type=jnp.float32,
        )
        model_real = jnp.sum(picked[:rows] * row_weights, axis=0, keepdims=True)
        model_imag = jnp.sum(picked[rows:] * row_weights, axis=0, keepdims=True)
        cosine, sine = phase[0, at, :], phase[1, at, :]
        res_real = obs_ref[s, 0:1, :] - (model_real * cosine - model_imag * sine)
        res_imag = obs_ref[s, 1:2, :] - (model_real * sine + model_imag * cosine)
        res_ref[s, 0:1, :] = res_real
        res_ref[s, 1:2, :] = res_imag
        w_real = res_real * cosine + res_imag * sine
        w_imag = res_imag * cosine - res_real * sine
        spread_rows = jnp.concatenate([row_weights * w_real, row_weights * w_imag], axis=0).astype(jnp.bfloat16)
        back = lax.dot_general(
            column_weights, spread_rows, (((1,), (1,)), ((), ())), preferred_element_type=jnp.float32
        )
        adj[0, where, :] = jnp.concatenate([back[:pairs, :rows], back[pairs:, :rows]], axis=1)
        adj[1, where, :] = jnp.concatenate([back[:pairs, rows:], back[pairs:, rows:]], axis=1)

    def four(block, carry):
        for k in range(4):
            one(4 * block + k)
        return carry

    lax.fori_loop(0, per // 4, four, 0)

    def gather(step, p, device, peer):
        block = out_ref.at[p, :, rows_of(device)]
        return remote(block, block, sg.at[step, p, device], dg.at[p, device], peer)

    def far(p, a, k):
        along = 1 - bits[p] if a else bits[p]
        across = 1 - bits[1 - p] if k else bits[1 - p]
        return 2 * compose(p, along, across) + core

    for p in range(2):
        for t in range(pairs):
            out_ref[p, t, rows_of(f)] = adj[p, pl.ds(t, per, stride=pairs), :].astype(jnp.bfloat16)
        gather(0, p, f, flip(1 - p)).start()
        gather(1, p, f, flip(p)).start()
        gather(2, p, f, other).start()
    for p in range(2):
        block = far(p, 0, 1)
        gather(0, p, block, flip(1 - p)).wait_recv()
        gather(1, p, block, flip(p)).start()
        gather(2, p, block, other).start()
    for k in range(2):
        for p in range(2):
            block = far(p, 1, k)
            gather(1, p, block, flip(p)).wait_recv()
            gather(2, p, block, other).start()
    for p in range(2):
        for h in range(4):
            gather(2, p, 2 * h + 1 - core, other).wait_recv()
    for p in range(2):
        for h in range(4):
            stage0(p, h).wait_send()
            gather(2, p, 2 * h + core, other).wait_send()
        for k in range(2):
            stage1(p, k).wait_send()
            gather(1, p, far(p, 0, k), flip(p)).wait_send()
        stage2(p).wait_send()
        gather(0, p, f, flip(1 - p)).wait_send()


def fused_middle(contrib, u, v, plane, observed, taps, table):
    _, pairs, subgrids, lanes = contrib.shape
    per, vis = u.shape
    vmem = pl.BlockSpec(memory_space=pltpu.VMEM)
    smem = pl.BlockSpec(memory_space=pltpu.SMEM)
    block = (pairs, per, lanes)
    wire = lambda *lead: pltpu.VMEM((*lead, *block), jnp.bfloat16)
    dma = lambda *shape: pltpu.SemaphoreType.DMA(shape)
    return pl.pallas_call(
        middle_kernel,
        out_shape=(
            jax.ShapeDtypeStruct((per, 2, vis), jnp.float32),
            jax.ShapeDtypeStruct(contrib.shape, jnp.bfloat16),
        ),
        in_specs=[vmem] * 5 + [smem] * 2,
        out_specs=(vmem, vmem),
        scratch_shapes=[
            wire(2, 4), wire(2, 4), wire(2, 2), wire(2, 2), wire(2),
            pltpu.VMEM((2, per * pairs, lanes), jnp.float32),
            pltpu.VMEM((2, per * pairs, lanes), jnp.float32),
            pltpu.VMEM((2, per, vis), jnp.float32),
            pltpu.VMEM((per, lanes // 2, vis), jnp.float32),
            pltpu.VMEM((per, 2 * pairs, vis), jnp.bfloat16),
            dma(2, 4), dma(2, 4), dma(2, 2), dma(2, 2), dma(2), dma(2), dma(3, 2, 8), dma(2, 8),
        ],
        compiler_params=pltpu.CompilerParams(collective_id=2, has_side_effects=True),
        name="degrid_exchange",
    )(contrib, u, v, plane, observed, taps, table)


def local(n, nf, model_strip, screen_angle, facet_window, facet_shift, kernel_taps, plane_angle, u_cell, v_cell, w_plane, observed):
    _, _, cols, length = screen_angle.shape
    per = u_cell.shape[1]
    subgrids = per * nf
    rows = length // subgrids
    block = rows // n
    vmem = pl.BlockSpec(memory_space=pltpu.VMEM)
    fr, fi = dft(rows)
    gr, gi = dft(subgrids)
    turn = 2.0 * np.pi * (np.arange(rows)[:, None] * np.arange(subgrids)[None, :] % length) / length
    twist = np.stack([np.cos(turn), -np.sin(turn)]).astype(np.float32)
    bf = lambda a: jnp.asarray(a.astype(np.float32)).astype(jnp.bfloat16)
    f1 = bf(np.block([[fr, -fi], [fi, fr]]))
    g1 = bf(np.block([[gr, -gi], [gi, gr]]))
    g2 = bf(np.block([[gr.T, gi.T], [-gi.T, gr.T]]))
    zero = np.zeros_like(fr)
    f2 = bf(
        np.block(
            [
                [fr.T, zero, fi.T, zero],
                [-fi.T, zero, fr.T, zero],
                [zero, fr.T, zero, fi.T],
                [zero, -fi.T, zero, fr.T],
            ]
        )
    )
    tw2 = np.ascontiguousarray(np.tile(np.swapaxes(twist, 1, 2), (1, 1, 2)))
    factor = facet_factor(facet_window[0], facet_shift[0], subgrids)
    x = model_strip[0].reshape(2, cols, block, subgrids).transpose(1, 0, 2, 3)
    angle = screen_angle[0, 0].reshape(cols, rows, subgrids)
    contrib = pl.pallas_call(
        functools.partial(forward_kernel, n),
        out_shape=jax.ShapeDtypeStruct((2, cols // 2, subgrids, 2 * rows), jnp.bfloat16),
        in_specs=[vmem] * 6,
        out_specs=vmem,
        scratch_shapes=[
            pltpu.VMEM((n, cols, 2, block, subgrids), jnp.bfloat16),
            pltpu.SemaphoreType.DMA((2, n - 1, CHUNKS)),
            pltpu.SemaphoreType.DMA((2, n - 1, CHUNKS)),
            pltpu.SemaphoreType.DMA,
        ],
        compiler_params=pltpu.CompilerParams(collective_id=0, has_side_effects=True),
        name="gather_forward",
    )(x, angle, f1, g1, jnp.asarray(twist), factor)
    if nf == 8 and per % 16 == 0:
        table = jnp.stack([jnp.cos(plane_angle[0]), jnp.sin(plane_angle[0])])
        residual, every = fused_middle(
            contrib, u_cell[0], v_cell[0], w_plane[0], observed[0], kernel_taps, table
        )
    else:
        parts = contrib.reshape(2, cols // 2, nf, per, 2 * rows)
        received = lax.all_to_all(parts, "facet", split_axis=2, concat_axis=2, tiled=True)
        grids = jnp.sum(received.astype(jnp.float32), axis=2)
        grids = grids.reshape(2, cols // 2, per, 2, rows).transpose(2, 1, 3, 0, 4).reshape(per, cols, 2 * rows)
        residual, adjoint = middle(
            grids, u_cell[0], v_cell[0], w_plane[0], observed[0], plane_angle[0], kernel_taps, rows, cols
        )
        adjoint = adjoint.reshape(per, cols // 2, 2, 2, rows).transpose(3, 1, 0, 2, 4).reshape(2, cols // 2, per, 2 * rows)
        every = lax.all_gather(adjoint, "facet", axis=2, tiled=True)
    gradient = pl.pallas_call(
        functools.partial(backward_kernel, n),
        out_shape=jax.ShapeDtypeStruct((cols, 2, block, subgrids), jnp.float32),
        in_specs=[vmem] * 6,
        out_specs=vmem,
        scratch_shapes=[
            pltpu.VMEM((n, cols, 2, block, subgrids), jnp.bfloat16),
            pltpu.VMEM((2, n, cols, 2, block, subgrids), jnp.bfloat16),
            pltpu.VMEM((2, n, cols, 2, block, subgrids), jnp.bfloat16),
            pltpu.SemaphoreType.DMA((2, n, CHUNKS)),
            pltpu.SemaphoreType.DMA((2, n, CHUNKS)),
        ],
        compiler_params=pltpu.CompilerParams(collective_id=1, has_side_effects=True),
        name="backward_scatter",
    )(every, angle, g2, f2, jnp.asarray(tw2), factor)
    gradient = gradient.transpose(1, 0, 2, 3).reshape(1, 2, cols, block * subgrids)
    return (residual[None], gradient)


def solution(mesh):
    return jax.shard_map(
        functools.partial(local, mesh.shape["layer"], mesh.shape["facet"]),
        mesh=mesh,
        in_specs=(
            P("facet", None, None, "layer"),
            P("layer", "facet", None, None),
            P("facet", None),
            P("facet"),
            P(),
            P("layer", None),
            P("layer", "facet", None),
            P("layer", "facet", None),
            P("layer", "facet", None),
            P("layer", "facet", None, None),
        ),
        out_specs=(P("layer", "facet", None, None), P("facet", None, None, "layer")),
        check_vma=False,
    )
```

profile of v0, /device:TPU:0, one launch (start us, length us, event | category | flops | bytes accessed | tf_op | source)
XLA Modules:
  0.0 139.1 jit_solution(2230505218648617970)
XLA Ops:
  0.6 0.0 copy-start
  1.4 0.7 fusion.3
  2.1 0.6 pad_maximum_fusion.2.table_ref
  2.7 0.5 broadcast.269
  3.2 1.5 %reduce.3 = f32[8192]{0:T(1024)S(1)} reduce(f32[1,8192]{1,0:T(1,128)} %param.18, f32[]{:T(128)} %broadcast.269), dimensions={0}, to_apply=%param.18.reduce_sub_computation.3 | reduce | bytes 65540 | tf_op args[2]
  4.7 0.1 concatenate.19
  4.7 0.4 cosine_multiply_fusion
  5.1 0.7 pad_maximum_fusion.fac_ref
  5.8 1.1 copy.23
  6.9 0.8 copy_bitcast_fusion.x_ref
  7.7 0.0 copy-done
  7.7 1.3 copy.24
  9.0 43.9 %gather_forward.1.contrib_ref = bf16[2,32,128,128]{3,2,1,0:T(8,128)(2,1)} custom-call(bf16[64,2,16,128]{3,2,1,0:T(8,128)(2,1)} %copy_bitcast_fusion.x_ref, bf16[64,64,128]{2,1,0:T(8,128)(2,1)} %bitcast.27, bf16[128,128]{1,0:T(8,128)(2,1)} %constant.57.f1_ref, bf16[256,256]{1,0:T(8,128)(2,1)} %constant.58.g_ref, f32[2,64,128]{2,1,0:T(8,128)} %constant.46.clone.tw_ref, ...), custom_call_target="tpu_custom_call" | custom-call | tf_op jit(solution)/shard_map/gather_forward/pallas_call | solution.py:553
  53.0 36.7 %degrid_exchange.1 = (f32[16,2,512]{2,1,0:T(2,128)}, bf16[2,32,128,128]{3,2,1,0:T(8,128)(2,1)}) custom-call(bf16[2,32,128,128]{3,2,1,0:T(8,128)(2,1)} %gather_forward.1.contrib_ref, s32[16,512]{1,0:T(8,128)} %bitcast.35, s32[16,512]{1,0:T(8,128)} %bitcast.36, s32[16,512]{1,0:T(8,128)} %bitcast.37, f32[16,2,512]{2,1,0:T(2,128)} %bitcast.33, f32[7]{0:T(128)} %taps_ref.1, ...), custom_call_target="tpu_custom_call" | custom-call | tf_op jit(solution)/shard_map/degrid_exchange/pallas_call | solution.py:501
  89.7 45.4 %backward_scatter.1 = f32[64,2,16,128]{3,2,1,0:T(8,128)} custom-call(bf16[2,32,128,128]{3,2,1,0:T(8,128)(2,1)} %get-tuple-element.5.a_ref, bf16[64,64,128]{2,1,0:T(8,128)(2,1)} %bitcast.28, bf16[256,256]{1,0:T(8,128)(2,1)} %constant.59.g_ref, bf16[256,256]{1,0:T(8,128)(2,1)} %constant.60.f2_ref, f32[2,128,128]{2,1,0:T(8,128)} %constant.47.clone.tw_ref, ...), custom_call_target="tpu_custom_call" | custom-call | tf_op jit(solution)/shard_map/backward_scatter/pallas_call | solution.py:582
  135.1 0.0 copy-start.1
  135.1 1.8 %reshape.288 = f32[1,2,64,2048]{3,1,2,0:T(2,128)S(1)} reshape(f32[2,64,16,128]{3,2,0,1:T(8,128)} %bitcast.29) | data formatting | bytes 2097152 | tf_op jit(solution)/shard_map/reshape | solution.py:597
  136.9 1.6 %copy.21 = f32[1,2,64,2048]{3,2,1,0:T(8,128)} copy(f32[1,2,64,2048]{3,1,2,0:T(2,128)S(1)} %reshape.288) | data formatting | bytes 2097152
  138.5 0.0 copy-done.1
  138.5 0.6 copy.28
  (3 shorter events, 0.0 us)
Async XLA Ops:
  0.6 7.1 %copy-start = (bf16[1,1,64,8192]{3,2,1,0:T(8,128)(2,1)S(1)}, bf16[1,1,64,8192]{3,2,1,0:T(8,128)(2,1)}, u32[]{:S(2)}) copy-start(bf16[1,1,64,8192]{3,2,1,0:T(8,128)(2,1)} %param.17) | copy-start | bytes 3145732
  135.1 3.4 %copy-start.1 = (f32[16,2,512]{2,1,0:T(2,128)S(1)}, f32[16,2,512]{2,1,0:T(2,128)}, u32[]{:S(2)}) copy-start(f32[16,2,512]{2,1,0:T(2,128)} %get-tuple-element.4) | copy-start | bytes 196612
where the time goes:
time: 139 us
  Pallas kernels  126 us (91%)
  local copies, waits for them, and re-layouts  8.52 us (6%)
  other arithmetic  3.08 us (2%)
  between operations  1.45 us (1%)
    pallas_call x1, Pallas kernels, local(): pl.pallas_call(functools.partial(backward_kernel, n), out_shape=jax.Shape...  45.4 us
    pallas_call x1, Pallas kernels, local(): pl.pallas_call(functools.partial(forward_kernel, n), out_shape=jax.ShapeD...  43.9 us
    pallas_call x1, Pallas kernels, fused_middle(): pl.pallas_call(middle_kernel, out_shape=(jax.ShapeDtypeStruct((per, 2, vi...  36.7 us
    unnamed x9, local copies, waits for them, and re-layouts  5.13 us

commit v1 on v0

--- a/solution.py
+++ b/solution.py
@@ -12,6 +12,7 @@
 MESH = pl.DeviceIdType.MESH
 BACK_GAIN = 8.0
 CHUNKS = 8
+MOVED = 3
 
 
 def _fit(values, degree):
@@ -307,109 +308,311 @@
     return jnp.stack([res_real, res_imag], axis=1), adjoint.astype(jnp.bfloat16)
 
 
-def middle_kernel(
-    contrib_ref, u_ref, v_ref, plane_ref, obs_ref, taps_ref, table_ref, res_ref, out_ref,
-    r0, acc0, r1, acc1, r2, fin, adj, phase, row_table, column_table, s0, d0, s1, d1, s2, d2, sg, dg,
+def fused_kernel(
+    n, moved, x_ref, ang_ref, win_ref, u_ref, v_ref, plane_ref, obs_ref, f1_ref, g1_ref, tw_ref, g2_ref, f2_ref, tw2_ref,
+    taps_ref, pang_ref, shift_ref, res_ref, out_ref,
+    buf, angb, cs, fac, tmpx, tmpa, contrib, r0, acc0, r1, acc1, r2, outbox, inbox, fin, adj, phase, row_table, column_table,
+    every, term, sbuf, rbuf, otmp,
+    fs, fr, angs, angr, s0, d0, s1, d1, s2, d2, xs, xr, ys, yr, sa, da, sb, db, sc, dc, bs, br,
 ):
-    pairs = contrib_ref.shape[1]
+    cols, rows = angb.shape[0] - cs_extra(moved, angb.shape[0]), angb.shape[1]
+    lanes = 2 * rows
+    subgrids = g1_ref.shape[0] // 2
+    block = rows // n
     per, vis = u_ref.shape
-    rows = contrib_ref.shape[3] // 2
-    cols = 2 * pairs
+    pairs = cols // 2
+    cq = cols // CHUNKS
+    pq = cq // 2
+    i = lax.axis_index("layer")
     f = lax.axis_index("facet")
     core = lax.rem(f, 2)
     chip = lax.div(f, 2)
     bits = (lax.rem(chip, 2), lax.div(chip, 2))
+    other = f + 1 - 2 * core
+    middle_layer = (i >= 1) & (i <= n - 2)
 
     def flip(b):
         return f + (1 - 2 * bits[b]) * (2 * (1 + b))
 
-    other = f + 1 - 2 * core
+    def near(step):
+        return jnp.clip(i + step, 0, n - 1)
+
+    inner = jnp.where(i == 0, 1, n - 2)
+    outer = jnp.where(i == 1, 0, n - 1)
+
     barrier = pltpu.get_barrier_semaphore()
     for peer in (other, flip(0), flip(1)):
         pl.semaphore_signal(barrier, inc=1, device_id={"facet": peer}, device_id_type=MESH)
-    pl.semaphore_wait(barrier, 3)
-
-    def rows_of(device):
-        return pl.ds(pl.multiple_of(device * per, per), per)
-
-    def compose(p, along, across):
-        return along + 2 * across if p == 0 else across + 2 * along
-
-    def remote(src, dst, send, recv, device):
+
+    @pl.when(i > 0)
+    def _():
+        pl.semaphore_signal(barrier, inc=1, device_id={"layer": i - 1}, device_id_type=MESH)
+
+    @pl.when(i < n - 1)
+    def _():
+        pl.semaphore_signal(barrier, inc=1, device_id={"layer": i + 1}, device_id_type=MESH)
+
+    pl.semaphore_wait(barrier, 3 + jnp.where(i > 0, 1, 0) + jnp.where(i < n - 1, 1, 0))
+
+    def is_moved(q):
+        return (lax.rem(q, 2) == 1) & (q < 2 * moved)
+
+    def bottom(q):
+        return jnp.where(is_moved(q), 1, 0)
+
+    def top(q):
+        return jnp.where(is_moved(q), n - 2, n - 1)
+
+    def has_own(q):
+        return (i >= bottom(q)) & (i <= top(q))
+
+    def has_extra(q):
+        return middle_layer & is_moved(q)
+
+    def remote(src, dst, send, recv, axis, device):
         return pltpu.make_async_remote_copy(
-            src_ref=src, dst_ref=dst, send_sem=send, recv_sem=recv,
-            device_id={"facet": device}, device_id_type=MESH,
+            src_ref=src, dst_ref=dst, send_sem=send, recv_sem=recv, device_id={axis: device}, device_id_type=MESH
         )
 
-    def stage0(p, h):
-        return remote(
-            contrib_ref.at[p, :, rows_of(2 * h + 1 - core)], r0.at[p, h], s0.at[p, h], d0.at[p, h], other
-        )
-
-    def stage1(p, k):
-        return remote(acc0.at[p, compose(p, 1 - bits[p], k)], r1.at[p, k], s1.at[p, k], d1.at[p, k], flip(p))
-
-    def stage2(p):
-        return remote(acc1.at[p, 1 - bits[1 - p]], r2.at[p], s2.at[p], d2.at[p], flip(1 - p))
-
-    def add0(p, h):
-        stage0(p, h).wait_recv()
-        mine = contrib_ref[p, :, rows_of(2 * h + core)].astype(jnp.float32)
-        acc0[p, h] = (mine + r0[p, h].astype(jnp.float32)).astype(jnp.bfloat16)
-
-    order = [(a, k, p) for a in (1, 0) for k in range(2) for p in range(2)]
-    for a, k, p in order:
-        stage0(p, compose(p, 1 - bits[p] if a else bits[p], k)).start()
-    for k in range(2):
+    def chunk(q):
+        return pl.ds(pl.multiple_of(q * cq, cq), cq)
+
+    def copy(direction, s, q):
+        step = 1 if direction == 0 else -1
+        origin = jnp.clip(i - step * s, 0, n - 1)
+        ref = buf.at[origin, chunk(q)]
+        return remote(ref, ref, fs.at[direction, s, q], fr.at[direction, s, q], "layer", near(step))
+
+    def sends(direction, s, q):
+        if direction == 0:
+            return (i - s >= 0) & (i + 1 <= top(q))
+        return (i + s <= n - 1) & (i - 1 >= bottom(q))
+
+    def gets(direction, s, q):
+        if direction == 0:
+            return (i - 1 - s >= 0) & (i <= top(q))
+        return (i + 1 + s <= n - 1) & (i >= bottom(q))
+
+    def send_own(q):
+        for d in range(2):
+            @pl.when(sends(d, 0, q))
+            def _():
+                copy(d, 0, q).start()
+
+    def angle_copy(m):
+        src = angb.at[chunk(2 * m + 1)]
+        dst = angb.at[chunk(CHUNKS + m)]
+        return remote(src, dst, angs.at[m], angr.at[m], "layer", inner)
+
+    def relayout(g, carry):
+        at = pl.ds(pl.multiple_of(g * 2 * cq, 2 * cq), 2 * cq)
         for p in range(2):
-            add0(p, compose(p, 1 - bits[p], k))
-            stage1(p, k).start()
-    for k in range(2):
-        for p in range(2):
-            add0(p, compose(p, bits[p], k))
+            v = x_ref[p, at, :].astype(jnp.float32)
+            for m in range(block):
+                tmpx[p, pl.ds(m, 2 * cq, stride=block), :] = v[:, m * subgrids : (m + 1) * subgrids]
+            buf[i, at, p] = tmpx[p].reshape(2 * cq, block, subgrids).astype(jnp.bfloat16)
+
+        @pl.when(jnp.logical_not(middle_layer))
+        def _():
+            send_own(2 * g)
+            send_own(2 * g + 1)
+
+        @pl.when(middle_layer & (g == 0))
+        def _():
+            send_own(0)
+
+        for m in range(rows):
+            piece = ang_ref[at, m * subgrids : (m + 1) * subgrids].astype(jnp.float32)
+            tmpa[pl.ds(m, 2 * cq, stride=rows), :] = piece
+        angb[at] = tmpa[...].reshape(2 * cq, rows, subgrids).astype(jnp.bfloat16)
+
+        if moved:
+            @pl.when(jnp.logical_not(middle_layer) & (g < moved))
+            def _():
+                angle_copy(g).start()
+
+        return carry
+
+    lax.fori_loop(0, CHUNKS // 2, relayout, 0)
+
+    window = win_ref[...]
+    rolled = pltpu.roll(window, rows, axis=1)
+    left = lax.broadcasted_iota(jnp.int32, window.shape, 1) < rows
+    fac[0, pl.ds(0, subgrids // 2, stride=2), :] = jnp.where(left, window, rolled)
+    fac[0, pl.ds(1, subgrids // 2, stride=2), :] = jnp.where(left, rolled, window)
+    grid = fac[0]
+    length = subgrids * rows
+    high = lax.broadcasted_iota(jnp.int32, grid.shape, 0)
+    low = lax.broadcasted_iota(jnp.int32, grid.shape, 1)
+    low = jnp.where(low < rows, low, low - rows)
+    turns = lax.rem((high * rows + low) * shift_ref[0], length)
+    turns = jnp.where(turns * 2 >= length, turns - length, turns)
+    cosine, sine = cos_sin(turns.astype(jnp.float32) * (2.0 * math.pi / length))
+    fac[0] = grid * cosine
+    fac[1] = -grid * sine
 
     plane = plane_ref[...]
-    cosine = jnp.zeros(plane.shape, jnp.float32)
-    sine = jnp.zeros(plane.shape, jnp.float32)
-    for k in range(table_ref.shape[1]):
-        hit = plane == k
-        cosine = jnp.where(hit, table_ref[0, k], cosine)
-        sine = jnp.where(hit, table_ref[1, k], sine)
+    angle = jnp.zeros(plane.shape, jnp.float32)
+    for k in range(pang_ref.shape[1]):
+        angle = jnp.where(plane == k, pang_ref[0, k], angle)
+    cosine, sine = cos_sin(angle)
     phase[0] = cosine
     phase[1] = sine
 
-    def weights(cells, position, length):
+    def weights(cells, position, size):
         count = taps_ref.shape[0]
         offset = position - cells + count // 2
-        offset = jnp.where(offset < 0, offset + length, jnp.where(offset >= length, offset - length, offset))
+        offset = jnp.where(offset < 0, offset + size, jnp.where(offset >= size, offset - size, offset))
         out = jnp.zeros(offset.shape, jnp.float32)
         for t in range(count):
             out = jnp.where(offset == t, taps_ref[t], out)
         return out
 
-    def prepare(s, carry):
+    def prepare(s):
         at = pl.ds(s, 1)
         row = lax.broadcasted_iota(jnp.int32, (rows, vis), 0)
         half = lax.broadcasted_iota(jnp.int32, (pairs, vis), 0)
         col = jnp.concatenate([2 * half, 2 * half + 1], axis=0)
         row_table[s] = weights(u_ref[at, :], row, rows)
         column_table[s] = weights(v_ref[at, :], col, cols).astype(jnp.bfloat16)
+
+    def place(p, device):
+        b0, b1 = (device // 2) % 2, device // 4
+        return (b0 * 2 + b1) if p == 0 else (b1 * 2 + b0)
+
+    def compute_forward(q, unit):
+        twr, twi = tw_ref[0], tw_ref[1]
+        facr, faci = fac[0], fac[1]
+        base = chunk(unit).start
+        for pair in range(pq):
+            halves = []
+            for c in (2 * pair, 2 * pair + 1):
+                col = q * cq + c
+                xr_ = jnp.concatenate([buf[l, col, 0] for l in range(n)], axis=0).astype(jnp.float32)
+                xi_ = jnp.concatenate([buf[l, col, 1] for l in range(n)], axis=0).astype(jnp.float32)
+                cosine, sine = cos_sin(angb[base + c].astype(jnp.float32))
+                cs[base + c, 0] = cosine
+                cs[base + c, 1] = sine
+                x = jnp.concatenate([xr_ * cosine - xi_ * sine, xr_ * sine + xi_ * cosine], axis=0)
+                h = jnp.dot(f1_ref[...], x.astype(jnp.bfloat16), preferred_element_type=jnp.float32)
+                hr, hi = h[:rows], h[rows:]
+                halves.append(
+                    jnp.concatenate([hr * twr - hi * twi, hr * twi + hi * twr], axis=1).astype(jnp.bfloat16)
+                )
+            both = jnp.concatenate(halves, axis=0)
+            spec = lax.dot_general(
+                g1_ref[...], both, (((1,), (1,)), ((), ())), preferred_element_type=jnp.float32
+            )
+            sr, si = spec[:subgrids], spec[subgrids:]
+            parts = ((sr * facr - si * faci).astype(jnp.bfloat16), (sr * faci + si * facr).astype(jnp.bfloat16))
+            for p in range(2):
+                for device in range(8):
+                    contrib[unit, device % 2, p, place(p, device), pair * per : (pair + 1) * per] = parts[p][
+                        device * per : (device + 1) * per
+                    ]
+
+    def stage0(unit):
+        return remote(contrib.at[unit, 1 - core], r0.at[unit], s0.at[unit], d0.at[unit], "facet", other)
+
+    def stage1(unit, p):
+        src = acc0.at[unit, p, pl.ds((1 - bits[p]) * 2, 2)]
+        return remote(src, r1.at[unit, p], s1.at[unit, p], d1.at[unit, p], "facet", flip(p))
+
+    def stage2(unit, p):
+        src = acc1.at[unit, p, 1 - bits[1 - p]]
+        return remote(src, r2.at[unit, p], s2.at[unit, p], d2.at[unit, p], "facet", flip(1 - p))
+
+    def result(m):
+        return remote(outbox.at[m], inbox.at[m], xs.at[m], xr.at[m], "layer", jnp.where(middle_layer, outer, inner))
+
+    def add0(unit):
+        stage0(unit).wait_recv()
+        for p in range(2):
+            total = contrib[unit, core, p].astype(jnp.float32) + r0[unit, p].astype(jnp.float32)
+            acc0[unit, p] = total.astype(jnp.bfloat16)
+            stage1(unit, p).start()
+
+    def add1(unit):
+        for p in range(2):
+            stage1(unit, p).wait_recv()
+            mine = acc0[unit, p, pl.ds(bits[p] * 2, 2)].astype(jnp.float32)
+            acc1[unit, p] = (mine + r1[unit, p].astype(jnp.float32)).astype(jnp.bfloat16)
+            stage2(unit, p).start()
+
+    def store_fin(p, q, total):
+        for t in range(pq):
+            fin[p, pl.ds(q * pq + t, per, stride=pairs), :] = total[t * per : (t + 1) * per]
+
+    def add2(q, unit, m):
+        for p in range(2):
+            stage2(unit, p).wait_recv()
+            total = acc1[unit, p, bits[1 - p]].astype(jnp.float32) + r2[unit, p].astype(jnp.float32)
+            if m is None:
+                store_fin(p, q, total)
+            else:
+                outbox[m, p] = total.astype(jnp.bfloat16)
+        if m is not None:
+            result(m).start()
+
+    def at_age(t, age, act):
+        q = t - (n - 1) - age
+        m = lax.div(q, 2)
+        live = (q >= 0) & (q < CHUNKS)
+
+        @pl.when(live & has_own(q))
+        def _():
+            act(q, q, None)
+
+        if moved:
+            @pl.when(live & has_extra(q))
+            def _():
+                act(q, CHUNKS + m, m)
+
+    def run_forward(q, unit, m):
+        if m is not None:
+            angle_copy(m).wait_recv()
+        compute_forward(q, unit)
+        stage0(unit).start()
+
+    def forward_step(t, carry):
+        @pl.when((t > 0) & (t < CHUNKS) & middle_layer)
+        def _():
+            send_own(t)
+
+        for s in range(n - 1):
+            q = t - 1 - s
+
+            @pl.when((q >= 0) & (q < CHUNKS))
+            def _():
+                for d in range(2):
+                    @pl.when(gets(d, s, q))
+                    def _():
+                        copy(d, s, q).wait_recv()
+                        if s + 1 < n - 1:
+                            @pl.when(sends(d, s + 1, q))
+                            def _():
+                                copy(d, s + 1, q).start()
+
+        @pl.when(t < per // 4)
+        def _():
+            for k in range(4):
+                prepare(4 * t + k)
+
+        at_age(t, 3, add2)
+        at_age(t, 2, lambda q, unit, m: add1(unit))
+        at_age(t, 1, lambda q, unit, m: add0(unit))
+        at_age(t, 0, run_forward)
         return carry
 
-    lax.fori_loop(0, per, prepare, 0)
-
-    for k in range(2):
-        for p in range(2):
-            stage1(p, k).wait_recv()
-            total = acc0[p, compose(p, bits[p], k)].astype(jnp.float32) + r1[p, k].astype(jnp.float32)
-            acc1[p, k] = total.astype(jnp.bfloat16)
-    for p in range(2):
-        stage2(p).start()
-    for p in range(2):
-        stage2(p).wait_recv()
-        for t in range(pairs):
-            total = acc1[p, bits[1 - p], t].astype(jnp.float32) + r2[p, t].astype(jnp.float32)
-            fin[p, pl.ds(t, per, stride=pairs), :] = total
+    lax.fori_loop(0, CHUNKS + n - 1 + 3, forward_step, 0)
+
+    if moved:
+        @pl.when(jnp.logical_not(middle_layer))
+        def _():
+            for m in range(moved):
+                result(m).wait_recv()
+                for p in range(2):
+                    store_fin(p, 2 * m + 1, inbox[m, p].astype(jnp.float32))
 
     def one(s):
         at = pl.ds(s, 1)
@@ -444,80 +647,301 @@
         adj[0, where, :] = jnp.concatenate([back[:pairs, :rows], back[pairs:, :rows]], axis=1)
         adj[1, where, :] = jnp.concatenate([back[:pairs, rows:], back[pairs:, rows:]], axis=1)
 
-    def four(block, carry):
+    def four(step, carry):
         for k in range(4):
-            one(4 * block + k)
+            one(4 * step + k)
         return carry
 
     lax.fori_loop(0, per // 4, four, 0)
 
-    def gather(step, p, device, peer):
-        block = out_ref.at[p, :, rows_of(device)]
-        return remote(block, block, sg.at[step, p, device], dg.at[p, device], peer)
-
-    def far(p, a, k):
-        along = 1 - bits[p] if a else bits[p]
-        across = 1 - bits[1 - p] if k else bits[1 - p]
-        return 2 * compose(p, along, across) + core
-
-    for p in range(2):
-        for t in range(pairs):
-            out_ref[p, t, rows_of(f)] = adj[p, pl.ds(t, per, stride=pairs), :].astype(jnp.bfloat16)
-        gather(0, p, f, flip(1 - p)).start()
-        gather(1, p, f, flip(p)).start()
-        gather(2, p, f, other).start()
-    for p in range(2):
-        block = far(p, 0, 1)
-        gather(0, p, block, flip(1 - p)).wait_recv()
-        gather(1, p, block, flip(p)).start()
-        gather(2, p, block, other).start()
-    for k in range(2):
+    def slot(p):
+        return bits[p] * 2 + bits[1 - p]
+
+    def own_block(unit, p):
+        return every.at[unit, p, core, slot(p)]
+
+    def give(m, p):
+        ref = own_block(CHUNKS + m, p)
+        return remote(ref, ref, ys.at[m, p], yr.at[m, p], "layer", jnp.where(middle_layer, outer, inner))
+
+    def gather_a(unit, p):
+        ref = own_block(unit, p)
+        return remote(ref, ref, sa.at[unit, p], da.at[unit, p], "facet", flip(1 - p))
+
+    def gather_b(unit, p):
+        ref = every.at[unit, p, core, pl.ds(bits[p] * 2, 2)]
+        return remote(ref, ref, sb.at[unit, p], db.at[unit, p], "facet", flip(p))
+
+    def gather_c(unit, p):
+        ref = every.at[unit, p, core]
+        return remote(ref, ref, sc.at[unit, p], dc.at[unit, p], "facet", other)
+
+    def fill(unit, q):
         for p in range(2):
-            block = far(p, 1, k)
-            gather(1, p, block, flip(p)).wait_recv()
-            gather(2, p, block, other).start()
-    for p in range(2):
-        for h in range(4):
-            gather(2, p, 2 * h + 1 - core, other).wait_recv()
-    for p in range(2):
-        for h in range(4):
-            stage0(p, h).wait_send()
-            gather(2, p, 2 * h + core, other).wait_send()
-        for k in range(2):
-            stage1(p, k).wait_send()
-            gather(1, p, far(p, 0, k), flip(p)).wait_send()
-        stage2(p).wait_send()
-        gather(0, p, f, flip(1 - p)).wait_send()
-
-
-def fused_middle(contrib, u, v, plane, observed, taps, table):
-    _, pairs, subgrids, lanes = contrib.shape
+            for t in range(pq):
+                piece = adj[p, pl.ds(q * pq + t, per, stride=pairs), :].astype(jnp.bfloat16)
+                every[unit, p, core, slot(p), t * per : (t + 1) * per] = piece
+
+    def fill_step(q, carry):
+        @pl.when(has_own(q))
+        def _():
+            fill(q, q)
+            for p in range(2):
+                gather_a(q, p).start()
+
+        if moved:
+            @pl.when(jnp.logical_not(has_own(q)))
+            def _():
+                m = lax.div(q, 2)
+                fill(CHUNKS + m, q)
+                for p in range(2):
+                    give(m, p).start()
+
+        return carry
+
+    lax.fori_loop(0, CHUNKS, fill_step, 0)
+
+    def back_copy(direction, j, q):
+        step = 1 if direction == 0 else -1
+        return remote(
+            sbuf.at[direction, j, chunk(q)], rbuf.at[direction, j, chunk(q)],
+            bs.at[direction, j, q], br.at[direction, j, q], "layer", near(step),
+        )
+
+    def behind(direction, q):
+        return i > bottom(q) if direction == 0 else i < top(q)
+
+    def compute_backward(q, unit, m):
+        twr, twi = tw2_ref[0], tw2_ref[1]
+        facr, faci = fac[0], fac[1]
+        base = chunk(unit).start
+        for pair in range(pq):
+            where = slice(pair * per, (pair + 1) * per)
+            grids = [
+                jnp.concatenate(
+                    [every[unit, p, device % 2, place(p, device), where] for device in range(8)], axis=0
+                ).astype(jnp.float32)
+                for p in range(2)
+            ]
+            ar, ai = grids
+            b = jnp.concatenate([ar * facr + ai * faci, ai * facr - ar * faci], axis=0).astype(jnp.bfloat16)
+            h = jnp.dot(g2_ref[...], b, preferred_element_type=jnp.float32)
+            hr, hi = h[:subgrids], h[subgrids:]
+            mixed = jnp.concatenate([hr * twr + hi * twi, hi * twr - hr * twi], axis=1).astype(jnp.bfloat16)
+            image = lax.dot_general(
+                f2_ref[...], mixed, (((1,), (1,)), ((), ())), preferred_element_type=jnp.float32
+            )
+            for c in range(2):
+                col = q * cq + 2 * pair + c
+                ir = image[2 * c * rows : (2 * c + 1) * rows]
+                ii = image[(2 * c + 1) * rows : (2 * c + 2) * rows]
+                cosine, sine = cs[base + 2 * pair + c, 0], cs[base + 2 * pair + c, 1]
+                tr = (BACK_GAIN * (ir * cosine + ii * sine)).astype(jnp.bfloat16)
+                ti = (BACK_GAIN * (ii * cosine - ir * sine)).astype(jnp.bfloat16)
+                for l in range(n):
+                    for part, value in ((0, tr), (1, ti)):
+                        piece = value[l * block : (l + 1) * block]
+                        if m is not None:
+                            total = term[l, col, part].astype(jnp.float32) + piece.astype(jnp.float32)
+                            piece = total.astype(jnp.bfloat16)
+                        term[l, col, part] = piece
+
+    def run_backward(q, unit, m):
+        for p in range(2):
+            gather_c(unit, p).wait_recv()
+        compute_backward(q, unit, m)
+
+    def relay(direction, j, q):
+        where = chunk(q)
+
+        @pl.when(behind(direction, q))
+        def _():
+            back_copy(direction, j, q).wait_recv()
+            total = term[j, where].astype(jnp.float32) + rbuf[direction, j, where].astype(jnp.float32)
+            sbuf[direction, j, where] = total.astype(jnp.bfloat16)
+
+        @pl.when(jnp.logical_not(behind(direction, q)))
+        def _():
+            sbuf[direction, j, where] = term[j, where]
+
+        back_copy(direction, j, q).start()
+
+    def units_of(q, act):
+        live = (q >= 0) & (q < CHUNKS)
+
+        @pl.when(live & has_own(q))
+        def _():
+            act(q, q, None)
+
+        if moved:
+            @pl.when(live & has_extra(q))
+            def _():
+                m = lax.div(q, 2)
+                act(q, CHUNKS + m, m)
+
+    def to_b(q, unit, m):
+        for p in range(2):
+            gather_a(unit, p).wait_recv()
+            gather_b(unit, p).start()
+
+    def to_c(q, unit, m):
+        for p in range(2):
+            gather_b(unit, p).wait_recv()
+            gather_c(unit, p).start()
+
+    def backward_step(t, carry):
+        if moved:
+            early = t + 1
+
+            @pl.when((early < CHUNKS) & has_extra(early))
+            def _():
+                m = lax.div(early, 2)
+                for p in range(2):
+                    give(m, p).wait_recv()
+                    gather_a(CHUNKS + m, p).start()
+
+        units_of(t, to_b)
+        units_of(t - 1, to_c)
+        units_of(t - 2, run_backward)
+        now = t - 2
+        for direction in range(2):
+            q = now - i if direction == 0 else now - (n - 1 - i)
+
+            @pl.when((q >= 0) & (q < CHUNKS) & has_own(q))
+            def _():
+                for d in range(n - 1, 0, -1):
+                    j = i + d if direction == 0 else i - d
+
+                    @pl.when((j < n) & (j >= 0))
+                    def _():
+                        relay(direction, j, q)
+
+        last = now - (n - 1)
+
+        @pl.when(last >= 0)
+        def _():
+            where = chunk(last)
+
+            @pl.when(has_own(last))
+            def _():
+                for p in range(2):
+                    otmp[p] = term[i, where, p].astype(jnp.float32).reshape(cq * block, subgrids)
+
+            @pl.when(jnp.logical_not(has_own(last)))
+            def _():
+                otmp[...] = jnp.zeros(otmp.shape, jnp.float32)
+
+            for direction in range(2):
+                @pl.when(behind(direction, last))
+                def _():
+                    back_copy(direction, i, last).wait_recv()
+                    for p in range(2):
+                        got = rbuf[direction, i, where, p].astype(jnp.float32)
+                        otmp[p] += got.reshape(cq * block, subgrids)
+
+            for p in range(2):
+                for m in range(block):
+                    out_ref[p, where, m * subgrids : (m + 1) * subgrids] = otmp[p, pl.ds(m, cq, stride=block), :]
+
+        return carry
+
+    lax.fori_loop(0, CHUNKS + n - 1 + 2, backward_step, 0)
+
+    def drain_unit(unit):
+        stage0(unit).wait_send()
+        for p in range(2):
+            stage1(unit, p).wait_send()
+            stage2(unit, p).wait_send()
+            gather_a(unit, p).wait_send()
+            gather_b(unit, p).wait_send()
+            gather_c(unit, p).wait_send()
+
+    def drain(q, carry):
+        for d in range(2):
+            for s in range(n - 1):
+                @pl.when(sends(d, s, q))
+                def _():
+                    copy(d, s, q).wait_send()
+
+        @pl.when(has_own(q))
+        def _():
+            drain_unit(q)
+            for direction in range(2):
+                for d in range(1, n):
+                    j = i + d if direction == 0 else i - d
+
+                    @pl.when((j < n) & (j >= 0))
+                    def _():
+                        back_copy(direction, j, q).wait_send()
+
+        if moved:
+            m = lax.div(q, 2)
+
+            @pl.when(has_extra(q))
+            def _():
+                drain_unit(CHUNKS + m)
+                result(m).wait_send()
+
+            @pl.when(is_moved(q) & jnp.logical_not(middle_layer))
+            def _():
+                angle_copy(m).wait_send()
+                for p in range(2):
+                    give(m, p).wait_send()
+
+        return carry
+
+    lax.fori_loop(0, CHUNKS, drain, 0)
+
+
+def cs_extra(moved, total):
+    return total * moved // (CHUNKS + moved)
+
+
+def fused(n, moved, x, angle, window, u, v, plane, observed, tables, taps, plane_angle, shift):
+    _, cols, _ = x.shape
     per, vis = u.shape
+    subgrids = tables[1].shape[0] // 2
+    rows = tables[0].shape[0] // 2
+    block = rows // n
+    pairs = cols // 2
+    cq = cols // CHUNKS
+    units = CHUNKS + moved
+    slab = (cq // 2) * per
+    lanes = 2 * rows
     vmem = pl.BlockSpec(memory_space=pltpu.VMEM)
     smem = pl.BlockSpec(memory_space=pltpu.SMEM)
-    block = (pairs, per, lanes)
-    wire = lambda *lead: pltpu.VMEM((*lead, *block), jnp.bfloat16)
+    bf = lambda *shape: pltpu.VMEM(shape, jnp.bfloat16)
+    f32 = lambda *shape: pltpu.VMEM(shape, jnp.float32)
     dma = lambda *shape: pltpu.SemaphoreType.DMA(shape)
+    box = max(moved, 1)
     return pl.pallas_call(
-        middle_kernel,
+        functools.partial(fused_kernel, n, moved),
         out_shape=(
             jax.ShapeDtypeStruct((per, 2, vis), jnp.float32),
-            jax.ShapeDtypeStruct(contrib.shape, jnp.bfloat16),
+            jax.ShapeDtypeStruct(x.shape, jnp.float32),
         ),
-        in_specs=[vmem] * 5 + [smem] * 2,
+        in_specs=[vmem] * 13 + [smem] * 3,
         out_specs=(vmem, vmem),
         scratch_shapes=[
-            wire(2, 4), wire(2, 4), wire(2, 2), wire(2, 2), wire(2),
-            pltpu.VMEM((2, per * pairs, lanes), jnp.float32),
-            pltpu.VMEM((2, per * pairs, lanes), jnp.float32),
-            pltpu.VMEM((2, per, vis), jnp.float32),
-            pltpu.VMEM((per, lanes // 2, vis), jnp.float32),
-            pltpu.VMEM((per, 2 * pairs, vis), jnp.bfloat16),
-            dma(2, 4), dma(2, 4), dma(2, 2), dma(2, 2), dma(2), dma(2), dma(3, 2, 8), dma(2, 8),
+            bf(n, cols, 2, block, subgrids), bf(cq * units, rows, subgrids), f32(cq * units, 2, rows, subgrids),
+            f32(2, subgrids, lanes), f32(2, 2 * cq * block, subgrids), f32(2 * cq * rows, subgrids),
+            bf(units, 2, 2, 4, slab, lanes), bf(units, 2, 4, slab, lanes), bf(units, 2, 4, slab, lanes),
+            bf(units, 2, 2, slab, lanes), bf(units, 2, 2, slab, lanes), bf(units, 2, slab, lanes),
+            bf(box, 2, slab, lanes), bf(box, 2, slab, lanes),
+            f32(2, per * pairs, lanes), f32(2, per * pairs, lanes), f32(2, per, vis),
+            f32(per, rows, vis), bf(per, cols, vis),
+            bf(units, 2, 2, 4, slab, lanes), bf(n, cols, 2, block, subgrids),
+            bf(2, n, cols, 2, block, subgrids), bf(2, n, cols, 2, block, subgrids), f32(2, cq * block, subgrids),
+            dma(2, n - 1, CHUNKS), dma(2, n - 1, CHUNKS), dma(box), dma(box),
+            dma(units), dma(units), dma(units, 2), dma(units, 2), dma(units, 2), dma(units, 2), dma(box), dma(box),
+            dma(box, 2), dma(box, 2), dma(units, 2), dma(units, 2), dma(units, 2), dma(units, 2), dma(units, 2), dma(units, 2),
+            dma(2, n, CHUNKS), dma(2, n, CHUNKS),
         ],
-        compiler_params=pltpu.CompilerParams(collective_id=2, has_side_effects=True),
-        name="degrid_exchange",
-    )(contrib, u, v, plane, observed, taps, table)
+        compiler_params=pltpu.CompilerParams(
+            collective_id=2, has_side_effects=True, vmem_limit_bytes=60 * 1024 * 1024
+        ),
+        name="fused_column",
+    )(x, angle, window, u, v, plane, observed, *tables, taps, plane_angle, shift)
 
 
 def local(n, nf, model_strip, screen_angle, facet_window, facet_shift, kernel_taps, plane_angle, u_cell, v_cell, w_plane, observed):
@@ -547,6 +971,13 @@
         )
     )
     tw2 = np.ascontiguousarray(np.tile(np.swapaxes(twist, 1, 2), (1, 1, 2)))
+    if nf == 8 and n == 4 and per % 16 == 0 and 2 * rows == subgrids == 128 and cols % (2 * CHUNKS) == 0:
+        tables = (f1, g1, jnp.asarray(twist), g2, f2, jnp.asarray(tw2))
+        residual, gradient = fused(
+            n, MOVED, model_strip[0], screen_angle[0, 0], facet_window.reshape(length // subgrids, subgrids),
+            u_cell[0], v_cell[0], w_plane[0], observed[0], tables, kernel_taps, plane_angle, facet_shift,
+        )
+        return (residual[None], gradient[None])
     factor = facet_factor(facet_window[0], facet_shift[0], subgrids)
     x = model_strip[0].reshape(2, cols, block, subgrids).transpose(1, 0, 2, 3)
     angle = screen_angle[0, 0].reshape(cols, rows, subgrids)
@@ -564,21 +995,15 @@
         compiler_params=pltpu.CompilerParams(collective_id=0, has_side_effects=True),
         name="gather_forward",
     )(x, angle, f1, g1, jnp.asarray(twist), factor)
-    if nf == 8 and per % 16 == 0:
-        table = jnp.stack([jnp.cos(plane_angle[0]), jnp.sin(plane_angle[0])])
-        residual, every = fused_middle(
-            contrib, u_cell[0], v_cell[0], w_plane[0], observed[0], kernel_taps, table
-        )
-    else:
-        parts = contrib.reshape(2, cols // 2, nf, per, 2 * rows)
-        received = lax.all_to_all(parts, "facet", split_axis=2, concat_axis=2, tiled=True)
-        grids = jnp.sum(received.astype(jnp.float32), axis=2)
-        grids = grids.reshape(2, cols // 2, per, 2, rows).transpose(2, 1, 3, 0, 4).reshape(per, cols, 2 * rows)
-        residual, adjoint = middle(
-            grids, u_cell[0], v_cell[0], w_plane[0], observed[0], plane_angle[0], kernel_taps, rows, cols
-        )
-        adjoint = adjoint.reshape(per, cols // 2, 2, 2, rows).transpose(3, 1, 0, 2, 4).reshape(2, cols // 2, per, 2 * rows)
-        every = lax.all_gather(adjoint, "facet", axis=2, tiled=True)
+    parts = contrib.reshape(2, cols // 2, nf, per, 2 * rows)
+    received = lax.all_to_all(parts, "facet", split_axis=2, concat_axis=2, tiled=True)
+    grids = jnp.sum(received.astype(jnp.float32), axis=2)
+    grids = grids.reshape(2, cols // 2, per, 2, rows).transpose(2, 1, 3, 0, 4).reshape(per, cols, 2 * rows)
+    residual, adjoint = middle(
+        grids, u_cell[0], v_cell[0], w_plane[0], observed[0], plane_angle[0], kernel_taps, rows, cols
+    )
+    adjoint = adjoint.reshape(per, cols // 2, 2, 2, rows).transpose(3, 1, 0, 2, 4).reshape(2, cols // 2, per, 2 * rows)
+    every = lax.all_gather(adjoint, "facet", axis=2, tiled=True)
     gradient = pl.pallas_call(
         functools.partial(backward_kernel, n),
         out_shape=jax.ShapeDtypeStruct((cols, 2, block, subgrids), jnp.float32),

time: 139 us -> 104 us (0.75)
  Pallas kernels: 126 us -> 98.8 us
  local copies, waits for them, and re-layouts: 8.52 us -> 3.77 us
  other arithmetic: 3.08 us -> 0 us
    pallas_call x3 -> x1, Pallas kernels: 126 us -> 98.8 us  [fused(): pl.pallas_call(functools.partial(fused_kernel, n, moved), out_shape=(jax....]
    reshape x1 -> x0, local copies, waits for them, and re-layouts: 1.79 us -> none  [local(): gradient.transpose(1, 0, 2, 3).reshape(1, 2, cols, block * subgrids)]
    unnamed x1 -> x0, other arithmetic: 1.48 us -> none
    unnamed x9 -> x2, local copies, waits for them, and re-layouts: 5.13 us -> 3.77 us
where the time goes in v1:
time: 104 us
  Pallas kernels  98.8 us (95%)
  local copies, waits for them, and re-layouts  3.77 us (4%)
  between operations  1.29 us (1%)
    pallas_call x1, Pallas kernels, fused(): pl.pallas_call(functools.partial(fused_kernel, n, moved), out_shape=(jax....  98.8 us
    unnamed x2, local copies, waits for them, and re-layouts  3.77 us

profile of v1, /device:TPU:0, one launch (start us, length us, event | category | flops | bytes accessed | tf_op | source)
XLA Modules:
  0.0 103.9 jit_solution(3106635194373784576)
XLA Ops:
  1.3 98.8 %fused_column.1 = (f32[16,2,512]{2,1,0:T(2,128)}, f32[2,64,2048]{2,1,0:T(8,128)}) custom-call(bf16[2,64,2048]{2,1,0:T(8,128)(2,1)} %bitcast.11, bf16[64,8192]{1,0:T(8,128)(2,1)} %bitcast.9, f32[64,128]{1,0:T(8,128)} %bitcast.14, s32[16,512]{1,0:T(8,128)} %bitcast.15, s32[16,512]{1,0:T(8,128)} %bitcast.16, s32[16,512]{1,0:T(8,128)} %bitcast.17, ...), custom_call_target="tpu_custom_call" | custom-call | tf_op jit(solution)/shard_map/fused_column/pallas_call | solution.py:917
  100.1 1.5 %copy.21 = f32[1,16,2,512]{3,2,1,0:T(2,128)} copy(f32[1,16,2,512]{3,2,1,0:T(2,128)} %bitcast.13) | data formatting | bytes 131072
  101.6 2.3 %copy.22 = f32[1,2,64,2048]{3,2,1,0:T(8,128)} copy(f32[1,2,64,2048]{3,2,1,0:T(8,128)} %bitcast.10) | data formatting | bytes 2097152

commit v2 on v1

--- a/solution.py
+++ b/solution.py
@@ -13,6 +13,13 @@
 BACK_GAIN = 8.0
 CHUNKS = 8
 MOVED = 3
+FIRST = 1
+EARLY = 1
+LEAD = 1
+HOP = 2
+AGES = (1, 3, 5)
+SPREAD = (2, 3)
+LAG = 2
 
 
 def _fit(values, degree):
@@ -355,7 +362,10 @@
     pl.semaphore_wait(barrier, 3 + jnp.where(i > 0, 1, 0) + jnp.where(i < n - 1, 1, 0))
 
     def is_moved(q):
-        return (lax.rem(q, 2) == 1) & (q < 2 * moved)
+        return (lax.rem(q, 2) == 1) & (q >= FIRST) & (q < FIRST + 2 * moved)
+
+    def moved_index(q):
+        return lax.div(q - FIRST, 2)
 
     def bottom(q):
         return jnp.where(is_moved(q), 1, 0)
@@ -381,7 +391,7 @@
         step = 1 if direction == 0 else -1
         origin = jnp.clip(i - step * s, 0, n - 1)
         ref = buf.at[origin, chunk(q)]
-        return remote(ref, ref, fs.at[direction, s, q], fr.at[direction, s, q], "layer", near(step))
+        return remote(ref, ref, fs.at[direction, s], fr.at[direction, s, q], "layer", near(step))
 
     def sends(direction, s, q):
         if direction == 0:
@@ -400,9 +410,9 @@
                 copy(d, 0, q).start()
 
     def angle_copy(m):
-        src = angb.at[chunk(2 * m + 1)]
+        src = angb.at[chunk(2 * m + FIRST)]
         dst = angb.at[chunk(CHUNKS + m)]
-        return remote(src, dst, angs.at[m], angr.at[m], "layer", inner)
+        return remote(src, dst, angs.at[0], angr.at[m], "layer", inner)
 
     def relayout(g, carry):
         at = pl.ds(pl.multiple_of(g * 2 * cq, 2 * cq), 2 * cq)
@@ -412,26 +422,30 @@
                 tmpx[p, pl.ds(m, 2 * cq, stride=block), :] = v[:, m * subgrids : (m + 1) * subgrids]
             buf[i, at, p] = tmpx[p].reshape(2 * cq, block, subgrids).astype(jnp.bfloat16)
 
+        for k in range(2):
+            @pl.when(jnp.logical_not(middle_layer) | (2 * g + k < LEAD))
+            def _():
+                send_own(2 * g + k)
+
         @pl.when(jnp.logical_not(middle_layer))
         def _():
-            send_own(2 * g)
-            send_own(2 * g + 1)
-
-        @pl.when(middle_layer & (g == 0))
-        def _():
-            send_own(0)
-
+            angle_relayout(g)
+
+        return carry
+
+    def angle_relayout(g):
+        at = pl.ds(pl.multiple_of(g * 2 * cq, 2 * cq), 2 * cq)
         for m in range(rows):
             piece = ang_ref[at, m * subgrids : (m + 1) * subgrids].astype(jnp.float32)
             tmpa[pl.ds(m, 2 * cq, stride=rows), :] = piece
         angb[at] = tmpa[...].reshape(2 * cq, rows, subgrids).astype(jnp.bfloat16)
 
         if moved:
-            @pl.when(jnp.logical_not(middle_layer) & (g < moved))
-            def _():
-                angle_copy(g).start()
-
-        return carry
+            m = g - FIRST // 2
+
+            @pl.when(jnp.logical_not(middle_layer) & (m >= 0) & (m < moved))
+            def _():
+                angle_copy(m).start()
 
     lax.fori_loop(0, CHUNKS // 2, relayout, 0)
 
@@ -512,18 +526,18 @@
                     ]
 
     def stage0(unit):
-        return remote(contrib.at[unit, 1 - core], r0.at[unit], s0.at[unit], d0.at[unit], "facet", other)
+        return remote(contrib.at[unit, 1 - core], r0.at[unit], s0.at[0], d0.at[unit], "facet", other)
 
     def stage1(unit, p):
         src = acc0.at[unit, p, pl.ds((1 - bits[p]) * 2, 2)]
-        return remote(src, r1.at[unit, p], s1.at[unit, p], d1.at[unit, p], "facet", flip(p))
+        return remote(src, r1.at[unit, p], s1.at[p], d1.at[unit, p], "facet", flip(p))
 
     def stage2(unit, p):
         src = acc1.at[unit, p, 1 - bits[1 - p]]
-        return remote(src, r2.at[unit, p], s2.at[unit, p], d2.at[unit, p], "facet", flip(1 - p))
+        return remote(src, r2.at[unit, p], s2.at[p], d2.at[unit, p], "facet", flip(1 - p))
 
     def result(m):
-        return remote(outbox.at[m], inbox.at[m], xs.at[m], xr.at[m], "layer", jnp.where(middle_layer, outer, inner))
+        return remote(outbox.at[m], inbox.at[m], xs.at[0], xr.at[m], "layer", jnp.where(middle_layer, outer, inner))
 
     def add0(unit):
         stage0(unit).wait_recv()
@@ -555,8 +569,8 @@
             result(m).start()
 
     def at_age(t, age, act):
-        q = t - (n - 1) - age
-        m = lax.div(q, 2)
+        q = t - ready - age
+        m = moved_index(q)
         live = (q >= 0) & (q < CHUNKS)
 
         @pl.when(live & has_own(q))
@@ -574,13 +588,19 @@
         compute_forward(q, unit)
         stage0(unit).start()
 
+    ready = 1 + HOP * (n - 2 - jnp.where(middle_layer, 1, 0))
+
     def forward_step(t, carry):
-        @pl.when((t > 0) & (t < CHUNKS) & middle_layer)
-        def _():
-            send_own(t)
+        @pl.when((t + LEAD < CHUNKS) & middle_layer)
+        def _():
+            send_own(t + LEAD)
+
+        @pl.when((t < CHUNKS // 2) & middle_layer)
+        def _():
+            angle_relayout(t)
 
         for s in range(n - 1):
-            q = t - 1 - s
+            q = t - 1 - HOP * s
 
             @pl.when((q >= 0) & (q < CHUNKS))
             def _():
@@ -598,13 +618,13 @@
             for k in range(4):
                 prepare(4 * t + k)
 
-        at_age(t, 3, add2)
-        at_age(t, 2, lambda q, unit, m: add1(unit))
-        at_age(t, 1, lambda q, unit, m: add0(unit))
+        at_age(t, AGES[2], add2)
+        at_age(t, AGES[1], lambda q, unit, m: add1(unit))
+        at_age(t, AGES[0], lambda q, unit, m: add0(unit))
         at_age(t, 0, run_forward)
         return carry
 
-    lax.fori_loop(0, CHUNKS + n - 1 + 3, forward_step, 0)
+    lax.fori_loop(0, CHUNKS + 1 + HOP * (n - 2) + AGES[2], forward_step, 0)
 
     if moved:
         @pl.when(jnp.logical_not(middle_layer))
@@ -612,7 +632,7 @@
             for m in range(moved):
                 result(m).wait_recv()
                 for p in range(2):
-                    store_fin(p, 2 * m + 1, inbox[m, p].astype(jnp.float32))
+                    store_fin(p, 2 * m + FIRST, inbox[m, p].astype(jnp.float32))
 
     def one(s):
         at = pl.ds(s, 1)
@@ -662,19 +682,19 @@
 
     def give(m, p):
         ref = own_block(CHUNKS + m, p)
-        return remote(ref, ref, ys.at[m, p], yr.at[m, p], "layer", jnp.where(middle_layer, outer, inner))
+        return remote(ref, ref, ys.at[0], yr.at[m, p], "layer", jnp.where(middle_layer, outer, inner))
 
     def gather_a(unit, p):
         ref = own_block(unit, p)
-        return remote(ref, ref, sa.at[unit, p], da.at[unit, p], "facet", flip(1 - p))
+        return remote(ref, ref, sa.at[p], da.at[unit, p], "facet", flip(1 - p))
 
     def gather_b(unit, p):
         ref = every.at[unit, p, core, pl.ds(bits[p] * 2, 2)]
-        return remote(ref, ref, sb.at[unit, p], db.at[unit, p], "facet", flip(p))
-
-    def gather_c(unit, p):
-        ref = every.at[unit, p, core]
-        return remote(ref, ref, sc.at[unit, p], dc.at[unit, p], "facet", other)
+        return remote(ref, ref, sb.at[p], db.at[unit, p], "facet", flip(p))
+
+    def gather_c(unit):
+        ref = every.at[unit, :, core]
+        return remote(ref, ref, sc.at[0], dc.at[unit], "facet", other)
 
     def fill(unit, q):
         for p in range(2):
@@ -692,7 +712,7 @@
         if moved:
             @pl.when(jnp.logical_not(has_own(q)))
             def _():
-                m = lax.div(q, 2)
+                m = moved_index(q)
                 fill(CHUNKS + m, q)
                 for p in range(2):
                     give(m, p).start()
@@ -705,7 +725,7 @@
         step = 1 if direction == 0 else -1
         return remote(
             sbuf.at[direction, j, chunk(q)], rbuf.at[direction, j, chunk(q)],
-            bs.at[direction, j, q], br.at[direction, j, q], "layer", near(step),
+            bs.at[direction, j], br.at[direction, j - 1 + direction, q], "layer", near(step),
         )
 
     def behind(direction, q):
@@ -747,8 +767,7 @@
                         term[l, col, part] = piece
 
     def run_backward(q, unit, m):
-        for p in range(2):
-            gather_c(unit, p).wait_recv()
+        gather_c(unit).wait_recv()
         compute_backward(q, unit, m)
 
     def relay(direction, j, q):
@@ -776,7 +795,7 @@
         if moved:
             @pl.when(live & has_extra(q))
             def _():
-                m = lax.div(q, 2)
+                m = moved_index(q)
                 act(q, CHUNKS + m, m)
 
     def to_b(q, unit, m):
@@ -787,36 +806,42 @@
     def to_c(q, unit, m):
         for p in range(2):
             gather_b(unit, p).wait_recv()
-            gather_c(unit, p).start()
+        gather_c(unit).start()
+
+    def pass_on(direction, q, inside):
+        kind = is_moved(q) if inside else jnp.logical_not(is_moved(q))
+
+        @pl.when((q >= 0) & (q < CHUNKS) & kind & has_own(q))
+        def _():
+            for d in range(n - 1, 0, -1):
+                j = i + d if direction == 0 else i - d
+
+                @pl.when((j < n) & (j >= 0))
+                def _():
+                    relay(direction, j, q)
 
     def backward_step(t, carry):
         if moved:
-            early = t + 1
+            early = t + EARLY
 
             @pl.when((early < CHUNKS) & has_extra(early))
             def _():
-                m = lax.div(early, 2)
+                m = moved_index(early)
                 for p in range(2):
                     give(m, p).wait_recv()
                     gather_a(CHUNKS + m, p).start()
 
         units_of(t, to_b)
-        units_of(t - 1, to_c)
-        units_of(t - 2, run_backward)
-        now = t - 2
+        units_of(t - SPREAD[0], to_c)
+        units_of(t - SPREAD[1], run_backward)
+        now = t - SPREAD[1]
         for direction in range(2):
-            q = now - i if direction == 0 else now - (n - 1 - i)
-
-            @pl.when((q >= 0) & (q < CHUNKS) & has_own(q))
-            def _():
-                for d in range(n - 1, 0, -1):
-                    j = i + d if direction == 0 else i - d
-
-                    @pl.when((j < n) & (j >= 0))
-                    def _():
-                        relay(direction, j, q)
-
-        last = now - (n - 1)
+            hops = i if direction == 0 else n - 1 - i
+            pass_on(direction, now - LAG * hops, False)
+            if moved:
+                pass_on(direction, now - LAG * (hops - 1), True)
+
+        last = now - LAG * (n - 1)
 
         @pl.when(last >= 0)
         def _():
@@ -845,52 +870,56 @@
 
         return carry
 
-    lax.fori_loop(0, CHUNKS + n - 1 + 2, backward_step, 0)
-
-    def drain_unit(unit):
-        stage0(unit).wait_send()
+    lax.fori_loop(0, CHUNKS + LAG * (n - 1) + SPREAD[1], backward_step, 0)
+
+    def sent(ref, sem):
+        remote(ref, ref, sem, angr.at[0], "facet", other).wait_send()
+
+    def drain(count):
+        some = pl.ds(0, count)
+        sent(contrib.at[some, 0], s0.at[0])
+        sent(every.at[some, :, 0], sc.at[0])
         for p in range(2):
-            stage1(unit, p).wait_send()
-            stage2(unit, p).wait_send()
-            gather_a(unit, p).wait_send()
-            gather_b(unit, p).wait_send()
-            gather_c(unit, p).wait_send()
-
-    def drain(q, carry):
-        for d in range(2):
-            for s in range(n - 1):
-                @pl.when(sends(d, s, q))
+            sent(r1.at[some, 0], s1.at[p])
+            sent(r2.at[some, 0], s2.at[p])
+            sent(every.at[some, 0, 0, 0], sa.at[p])
+            sent(every.at[some, 0, 0, pl.ds(0, 2)], sb.at[p])
+        chunks = min(count, CHUNKS)
+        for direction in range(2):
+            for d in range(1, n):
+                j = i + d if direction == 0 else i - d
+
+                @pl.when((j < n) & (j >= 0))
                 def _():
-                    copy(d, s, q).wait_send()
-
-        @pl.when(has_own(q))
-        def _():
-            drain_unit(q)
-            for direction in range(2):
-                for d in range(1, n):
-                    j = i + d if direction == 0 else i - d
-
-                    @pl.when((j < n) & (j >= 0))
-                    def _():
-                        back_copy(direction, j, q).wait_send()
-
+                    sent(sbuf.at[direction, 0, pl.ds(0, chunks * cq)], bs.at[direction, j])
+
+    for d in range(2):
+        target = i + 1 - 2 * d
+        inside = (target >= 1) & (target <= n - 2)
+        for s in range(n - 1):
+            origin = i - s if d == 0 else i + s
+            live = (origin >= 0) & (origin <= n - 1) & (target >= 0) & (target <= n - 1)
+
+            @pl.when(live & inside)
+            def _():
+                sent(buf.at[0], fs.at[d, s])
+
+            @pl.when(live & jnp.logical_not(inside))
+            def _():
+                sent(buf.at[0, pl.ds(0, (CHUNKS - moved) * cq)], fs.at[d, s])
+
+    @pl.when(middle_layer)
+    def _():
+        drain(CHUNKS + moved)
         if moved:
-            m = lax.div(q, 2)
-
-            @pl.when(has_extra(q))
-            def _():
-                drain_unit(CHUNKS + m)
-                result(m).wait_send()
-
-            @pl.when(is_moved(q) & jnp.logical_not(middle_layer))
-            def _():
-                angle_copy(m).wait_send()
-                for p in range(2):
-                    give(m, p).wait_send()
-
-        return carry
-
-    lax.fori_loop(0, CHUNKS, drain, 0)
+            sent(outbox, xs.at[0])
+
+    @pl.when(jnp.logical_not(middle_layer))
+    def _():
+        drain(CHUNKS - moved)
+        if moved:
+            sent(angb.at[pl.ds(0, moved * cq)], angs.at[0])
+            sent(every.at[pl.ds(0, moved), :, 0, 0], ys.at[0])
 
 
 def cs_extra(moved, total):
@@ -932,10 +961,10 @@
             f32(per, rows, vis), bf(per, cols, vis),
             bf(units, 2, 2, 4, slab, lanes), bf(n, cols, 2, block, subgrids),
             bf(2, n, cols, 2, block, subgrids), bf(2, n, cols, 2, block, subgrids), f32(2, cq * block, subgrids),
-            dma(2, n - 1, CHUNKS), dma(2, n - 1, CHUNKS), dma(box), dma(box),
-            dma(units), dma(units), dma(units, 2), dma(units, 2), dma(units, 2), dma(units, 2), dma(box), dma(box),
-            dma(box, 2), dma(box, 2), dma(units, 2), dma(units, 2), dma(units, 2), dma(units, 2), dma(units, 2), dma(units, 2),
-            dma(2, n, CHUNKS), dma(2, n, CHUNKS),
+            dma(2, n - 1), dma(2, n - 1, CHUNKS), dma(1), dma(box),
+            dma(1), dma(units), dma(2), dma(units, 2), dma(2), dma(units, 2), dma(1), dma(box),
+            dma(1), dma(box, 2), dma(2), dma(units, 2), dma(2), dma(units, 2), dma(1), dma(units),
+            dma(2, n), dma(2, n - 1, CHUNKS),
         ],
         compiler_params=pltpu.CompilerParams(
             collective_id=2, has_side_effects=True, vmem_limit_bytes=60 * 1024 * 1024

time: 104 us -> 95.2 us (0.915)
  Pallas kernels: 98.8 us -> 90 us
    pallas_call x1, Pallas kernels: 98.8 us -> 90 us  [fused(): pl.pallas_call(functools.partial(fused_kernel, n, moved), out_shape=(jax....]
where the time goes in v2:
time: 95.2 us; the launch traced here: 95 us
  Pallas kernels  90 us (95%)
  local copies, waits for them, and re-layouts  3.77 us (4%)
  between operations  1.29 us (1%)
    pallas_call x1, Pallas kernels, fused(): pl.pallas_call(functools.partial(fused_kernel, n, moved), out_shape=(jax....  90 us
    unnamed x2, local copies, waits for them, and re-layouts  3.77 us

profile of v2, /device:TPU:0, one launch (start us, length us, event | category | flops | bytes accessed | tf_op | source)
XLA Modules:
  0.0 95.0 jit_solution(4140696960061072001)
XLA Ops:
  1.3 90.0 %fused_column.1 = (f32[16,2,512]{2,1,0:T(2,128)}, f32[2,64,2048]{2,1,0:T(8,128)}) custom-call(bf16[2,64,2048]{2,1,0:T(8,128)(2,1)} %bitcast.11, bf16[64,8192]{1,0:T(8,128)(2,1)} %bitcast.9, f32[64,128]{1,0:T(8,128)} %bitcast.14, s32[16,512]{1,0:T(8,128)} %bitcast.15, s32[16,512]{1,0:T(8,128)} %bitcast.16, s32[16,512]{1,0:T(8,128)} %bitcast.17, ...), custom_call_target="tpu_custom_call" | custom-call | tf_op jit(solution)/shard_map/fused_column/pallas_call | solution.py:946
  91.2 1.5 %copy.21 = f32[1,16,2,512]{3,2,1,0:T(2,128)} copy(f32[1,16,2,512]{3,2,1,0:T(2,128)} %bitcast.13) | data formatting | bytes 131072
  92.7 2.3 %copy.22 = f32[1,2,64,2048]{3,2,1,0:T(8,128)} copy(f32[1,2,64,2048]{3,2,1,0:T(8,128)} %bitcast.10) | data formatting | bytes 2097152

commit v3 on v2

--- a/solution.py
+++ b/solution.py
@@ -13,12 +13,12 @@
 BACK_GAIN = 8.0
 CHUNKS = 8
 MOVED = 3
-FIRST = 1
-EARLY = 1
+FIRST = 3
+EARLY = 2
 LEAD = 1
 HOP = 2
-AGES = (1, 3, 5)
-SPREAD = (2, 3)
+AGES = (1, 3)
+SPREAD = 1
 LAG = 2
 
 
@@ -316,12 +316,18 @@
 
 
 def fused_kernel(
-    n, moved, x_ref, ang_ref, win_ref, u_ref, v_ref, plane_ref, obs_ref, f1_ref, g1_ref, tw_ref, g2_ref, f2_ref, tw2_ref,
-    taps_ref, pang_ref, shift_ref, res_ref, out_ref,
-    buf, angb, cs, fac, tmpx, tmpa, contrib, r0, acc0, r1, acc1, r2, outbox, inbox, fin, adj, phase, row_table, column_table,
+    n, moved, *refs,
+):
+    sources, (taps_ref, pang_ref, shift_ref, res_ref, out_ref), held = refs[:13], refs[13:18], refs[18:31]
+    (x_ref, ang_ref, win_ref, u_ref, v_ref, plane_ref, obs_ref, f1_ref, g1_ref, tw_ref, g2_ref, f2_ref, tw2_ref) = held
+    (
+    buf, angb, cs, fac, tmpx, tmpa, contrib, r0, acc0, r1, outbox, inbox, fin, adj, phase, row_table, column_table,
     every, term, sbuf, rbuf, otmp,
-    fs, fr, angs, angr, s0, d0, s1, d1, s2, d2, xs, xr, ys, yr, sa, da, sb, db, sc, dc, bs, br,
-):
+    fs, fr, angs, angr, s0, d0, s1, d1, xs, xr, ys, yr, sa, da, sc, dc, bs, br, load,
+    ) = refs[31:]
+    loads = [pltpu.make_async_copy(a, b, load.at[k]) for k, (a, b) in enumerate(zip(sources, held))]
+    for one_load in loads:
+        one_load.start()
     cols, rows = angb.shape[0] - cs_extra(moved, angb.shape[0]), angb.shape[1]
     lanes = 2 * rows
     subgrids = g1_ref.shape[0] // 2
@@ -338,8 +344,13 @@
     other = f + 1 - 2 * core
     middle_layer = (i >= 1) & (i <= n - 2)
 
-    def flip(b):
-        return f + (1 - 2 * bits[b]) * (2 * (1 + b))
+    def chip_of(k):
+        b0 = 1 - bits[0] if k & 1 else bits[0]
+        b1 = 1 - bits[1] if k & 2 else bits[1]
+        return b0 + 2 * b1
+
+    def peer_of(k):
+        return 2 * chip_of(k) + core
 
     def near(step):
         return jnp.clip(i + step, 0, n - 1)
@@ -348,7 +359,7 @@
     outer = jnp.where(i == 1, 0, n - 1)
 
     barrier = pltpu.get_barrier_semaphore()
-    for peer in (other, flip(0), flip(1)):
+    for peer in (other, peer_of(1), peer_of(2), peer_of(3)):
         pl.semaphore_signal(barrier, inc=1, device_id={"facet": peer}, device_id_type=MESH)
 
     @pl.when(i > 0)
@@ -359,7 +370,7 @@
     def _():
         pl.semaphore_signal(barrier, inc=1, device_id={"layer": i + 1}, device_id_type=MESH)
 
-    pl.semaphore_wait(barrier, 3 + jnp.where(i > 0, 1, 0) + jnp.where(i < n - 1, 1, 0))
+    pl.semaphore_wait(barrier, 4 + jnp.where(i > 0, 1, 0) + jnp.where(i < n - 1, 1, 0))
 
     def is_moved(q):
         return (lax.rem(q, 2) == 1) & (q >= FIRST) & (q < FIRST + 2 * moved)
@@ -447,7 +458,11 @@
             def _():
                 angle_copy(m).start()
 
+    loads[0].wait()
+    loads[1].wait()
     lax.fori_loop(0, CHUNKS // 2, relayout, 0)
+    for one_load in loads[2:]:
+        one_load.wait()
 
     window = win_ref[...]
     rolled = pltpu.roll(window, rows, axis=1)
@@ -489,10 +504,6 @@
         col = jnp.concatenate([2 * half, 2 * half + 1], axis=0)
         row_table[s] = weights(u_ref[at, :], row, rows)
         column_table[s] = weights(v_ref[at, :], col, cols).astype(jnp.bfloat16)
-
-    def place(p, device):
-        b0, b1 = (device // 2) % 2, device // 4
-        return (b0 * 2 + b1) if p == 0 else (b1 * 2 + b0)
 
     def compute_forward(q, unit):
         twr, twi = tw_ref[0], tw_ref[1]
@@ -521,46 +532,38 @@
             parts = ((sr * facr - si * faci).astype(jnp.bfloat16), (sr * faci + si * facr).astype(jnp.bfloat16))
             for p in range(2):
                 for device in range(8):
-                    contrib[unit, device % 2, p, place(p, device), pair * per : (pair + 1) * per] = parts[p][
+                    contrib[unit, device % 2, device // 2, p, pair * per : (pair + 1) * per] = parts[p][
                         device * per : (device + 1) * per
                     ]
 
     def stage0(unit):
         return remote(contrib.at[unit, 1 - core], r0.at[unit], s0.at[0], d0.at[unit], "facet", other)
 
-    def stage1(unit, p):
-        src = acc0.at[unit, p, pl.ds((1 - bits[p]) * 2, 2)]
-        return remote(src, r1.at[unit, p], s1.at[p], d1.at[unit, p], "facet", flip(p))
-
-    def stage2(unit, p):
-        src = acc1.at[unit, p, 1 - bits[1 - p]]
-        return remote(src, r2.at[unit, p], s2.at[p], d2.at[unit, p], "facet", flip(1 - p))
+    def stage1(unit, k):
+        src = acc0.at[unit, chip_of(k)]
+        return remote(src, r1.at[unit, k - 1], s1.at[k - 1], d1.at[unit, k - 1], "facet", peer_of(k))
 
     def result(m):
         return remote(outbox.at[m], inbox.at[m], xs.at[0], xr.at[m], "layer", jnp.where(middle_layer, outer, inner))
 
     def add0(unit):
         stage0(unit).wait_recv()
-        for p in range(2):
-            total = contrib[unit, core, p].astype(jnp.float32) + r0[unit, p].astype(jnp.float32)
-            acc0[unit, p] = total.astype(jnp.bfloat16)
-            stage1(unit, p).start()
-
-    def add1(unit):
-        for p in range(2):
-            stage1(unit, p).wait_recv()
-            mine = acc0[unit, p, pl.ds(bits[p] * 2, 2)].astype(jnp.float32)
-            acc1[unit, p] = (mine + r1[unit, p].astype(jnp.float32)).astype(jnp.bfloat16)
-            stage2(unit, p).start()
+        total = contrib[unit, core].astype(jnp.float32) + r0[unit].astype(jnp.float32)
+        acc0[unit] = total.astype(jnp.bfloat16)
+        for k in (3, 1, 2):
+            stage1(unit, k).start()
 
     def store_fin(p, q, total):
         for t in range(pq):
             fin[p, pl.ds(q * pq + t, per, stride=pairs), :] = total[t * per : (t + 1) * per]
 
     def add2(q, unit, m):
+        for k in (1, 2, 3):
+            stage1(unit, k).wait_recv()
         for p in range(2):
-            stage2(unit, p).wait_recv()
-            total = acc1[unit, p, bits[1 - p]].astype(jnp.float32) + r2[unit, p].astype(jnp.float32)
+            total = acc0[unit, chip, p].astype(jnp.float32)
+            for k in range(3):
+                total = total + r1[unit, k, p].astype(jnp.float32)
             if m is None:
                 store_fin(p, q, total)
             else:
@@ -618,13 +621,12 @@
             for k in range(4):
                 prepare(4 * t + k)
 
-        at_age(t, AGES[2], add2)
-        at_age(t, AGES[1], lambda q, unit, m: add1(unit))
+        at_age(t, AGES[1], add2)
         at_age(t, AGES[0], lambda q, unit, m: add0(unit))
         at_age(t, 0, run_forward)
         return carry
 
-    lax.fori_loop(0, CHUNKS + 1 + HOP * (n - 2) + AGES[2], forward_step, 0)
+    lax.fori_loop(0, CHUNKS + 1 + HOP * (n - 2) + AGES[1], forward_step, 0)
 
     if moved:
         @pl.when(jnp.logical_not(middle_layer))
@@ -674,48 +676,43 @@
 
     lax.fori_loop(0, per // 4, four, 0)
 
-    def slot(p):
-        return bits[p] * 2 + bits[1 - p]
-
-    def own_block(unit, p):
-        return every.at[unit, p, core, slot(p)]
-
-    def give(m, p):
-        ref = own_block(CHUNKS + m, p)
-        return remote(ref, ref, ys.at[0], yr.at[m, p], "layer", jnp.where(middle_layer, outer, inner))
-
-    def gather_a(unit, p):
-        ref = own_block(unit, p)
-        return remote(ref, ref, sa.at[p], da.at[unit, p], "facet", flip(1 - p))
-
-    def gather_b(unit, p):
-        ref = every.at[unit, p, core, pl.ds(bits[p] * 2, 2)]
-        return remote(ref, ref, sb.at[p], db.at[unit, p], "facet", flip(p))
-
-    def gather_c(unit):
-        ref = every.at[unit, :, core]
+    def own_block(unit):
+        return every.at[unit, core, chip]
+
+    def give(m):
+        ref = own_block(CHUNKS + m)
+        return remote(ref, ref, ys.at[0], yr.at[m], "layer", jnp.where(middle_layer, outer, inner))
+
+    def gather(unit, k):
+        ref = own_block(unit)
+        return remote(ref, ref, sa.at[k - 1], da.at[unit, k - 1], "facet", peer_of(k))
+
+    def gather_core(unit):
+        ref = every.at[unit, core]
         return remote(ref, ref, sc.at[0], dc.at[unit], "facet", other)
+
+    def spread_out(unit):
+        for k in (3, 1, 2):
+            gather(unit, k).start()
 
     def fill(unit, q):
         for p in range(2):
             for t in range(pq):
                 piece = adj[p, pl.ds(q * pq + t, per, stride=pairs), :].astype(jnp.bfloat16)
-                every[unit, p, core, slot(p), t * per : (t + 1) * per] = piece
+                every[unit, core, chip, p, t * per : (t + 1) * per] = piece
 
     def fill_step(q, carry):
         @pl.when(has_own(q))
         def _():
             fill(q, q)
-            for p in range(2):
-                gather_a(q, p).start()
+            spread_out(q)
 
         if moved:
             @pl.when(jnp.logical_not(has_own(q)))
             def _():
                 m = moved_index(q)
                 fill(CHUNKS + m, q)
-                for p in range(2):
-                    give(m, p).start()
+                give(m).start()
 
         return carry
 
@@ -739,7 +736,7 @@
             where = slice(pair * per, (pair + 1) * per)
             grids = [
                 jnp.concatenate(
-                    [every[unit, p, device % 2, place(p, device), where] for device in range(8)], axis=0
+                    [every[unit, device % 2, device // 2, p, where] for device in range(8)], axis=0
                 ).astype(jnp.float32)
                 for p in range(2)
             ]
@@ -767,7 +764,7 @@
                         term[l, col, part] = piece
 
     def run_backward(q, unit, m):
-        gather_c(unit).wait_recv()
+        gather_core(unit).wait_recv()
         compute_backward(q, unit, m)
 
     def relay(direction, j, q):
@@ -798,15 +795,10 @@
                 m = moved_index(q)
                 act(q, CHUNKS + m, m)
 
-    def to_b(q, unit, m):
-        for p in range(2):
-            gather_a(unit, p).wait_recv()
-            gather_b(unit, p).start()
-
-    def to_c(q, unit, m):
-        for p in range(2):
-            gather_b(unit, p).wait_recv()
-        gather_c(unit).start()
+    def to_core(q, unit, m):
+        for k in (1, 2, 3):
+            gather(unit, k).wait_recv()
+        gather_core(unit).start()
 
     def pass_on(direction, q, inside):
         kind = is_moved(q) if inside else jnp.logical_not(is_moved(q))
@@ -827,14 +819,12 @@
             @pl.when((early < CHUNKS) & has_extra(early))
             def _():
                 m = moved_index(early)
-                for p in range(2):
-                    give(m, p).wait_recv()
-                    gather_a(CHUNKS + m, p).start()
-
-        units_of(t, to_b)
-        units_of(t - SPREAD[0], to_c)
-        units_of(t - SPREAD[1], run_backward)
-        now = t - SPREAD[1]
+                give(m).wait_recv()
+                spread_out(CHUNKS + m)
+
+        units_of(t, to_core)
+        units_of(t - SPREAD, run_backward)
+        now = t - SPREAD
         for direction in range(2):
             hops = i if direction == 0 else n - 1 - i
             pass_on(direction, now - LAG * hops, False)
@@ -870,7 +860,7 @@
 
         return carry
 
-    lax.fori_loop(0, CHUNKS + LAG * (n - 1) + SPREAD[1], backward_step, 0)
+    lax.fori_loop(0, CHUNKS + LAG * (n - 1) + SPREAD, backward_step, 0)
 
     def sent(ref, sem):
         remote(ref, ref, sem, angr.at[0], "facet", other).wait_send()
@@ -878,12 +868,10 @@
     def drain(count):
         some = pl.ds(0, count)
         sent(contrib.at[some, 0], s0.at[0])
-        sent(every.at[some, :, 0], sc.at[0])
-        for p in range(2):
-            sent(r1.at[some, 0], s1.at[p])
-            sent(r2.at[some, 0], s2.at[p])
-            sent(every.at[some, 0, 0, 0], sa.at[p])
-            sent(every.at[some, 0, 0, pl.ds(0, 2)], sb.at[p])
+        sent(every.at[some, 0], sc.at[0])
+        for k in range(3):
+            sent(r1.at[some, 0], s1.at[k])
+            sent(every.at[some, 0, 0], sa.at[k])
         chunks = min(count, CHUNKS)
         for direction in range(2):
             for d in range(1, n):
@@ -919,7 +907,7 @@
         drain(CHUNKS - moved)
         if moved:
             sent(angb.at[pl.ds(0, moved * cq)], angs.at[0])
-            sent(every.at[pl.ds(0, moved), :, 0, 0], ys.at[0])
+            sent(every.at[pl.ds(0, moved), 0, 0], ys.at[0])
 
 
 def cs_extra(moved, total):
@@ -943,34 +931,36 @@
     f32 = lambda *shape: pltpu.VMEM(shape, jnp.float32)
     dma = lambda *shape: pltpu.SemaphoreType.DMA(shape)
     box = max(moved, 1)
+    arrays = (x, angle, window, u, v, plane, observed, *tables)
     return pl.pallas_call(
         functools.partial(fused_kernel, n, moved),
         out_shape=(
             jax.ShapeDtypeStruct((per, 2, vis), jnp.float32),
             jax.ShapeDtypeStruct(x.shape, jnp.float32),
         ),
-        in_specs=[vmem] * 13 + [smem] * 3,
+        in_specs=[pl.BlockSpec(memory_space=pltpu.HBM)] * 13 + [smem] * 3,
         out_specs=(vmem, vmem),
         scratch_shapes=[
+            *[pltpu.VMEM(a.shape, a.dtype) for a in arrays],
             bf(n, cols, 2, block, subgrids), bf(cq * units, rows, subgrids), f32(cq * units, 2, rows, subgrids),
             f32(2, subgrids, lanes), f32(2, 2 * cq * block, subgrids), f32(2 * cq * rows, subgrids),
-            bf(units, 2, 2, 4, slab, lanes), bf(units, 2, 4, slab, lanes), bf(units, 2, 4, slab, lanes),
-            bf(units, 2, 2, slab, lanes), bf(units, 2, 2, slab, lanes), bf(units, 2, slab, lanes),
+            bf(units, 2, 4, 2, slab, lanes), bf(units, 4, 2, slab, lanes), bf(units, 4, 2, slab, lanes),
+            bf(units, 3, 2, slab, lanes),
             bf(box, 2, slab, lanes), bf(box, 2, slab, lanes),
             f32(2, per * pairs, lanes), f32(2, per * pairs, lanes), f32(2, per, vis),
             f32(per, rows, vis), bf(per, cols, vis),
-            bf(units, 2, 2, 4, slab, lanes), bf(n, cols, 2, block, subgrids),
+            bf(units, 2, 4, 2, slab, lanes), bf(n, cols, 2, block, subgrids),
             bf(2, n, cols, 2, block, subgrids), bf(2, n, cols, 2, block, subgrids), f32(2, cq * block, subgrids),
             dma(2, n - 1), dma(2, n - 1, CHUNKS), dma(1), dma(box),
-            dma(1), dma(units), dma(2), dma(units, 2), dma(2), dma(units, 2), dma(1), dma(box),
-            dma(1), dma(box, 2), dma(2), dma(units, 2), dma(2), dma(units, 2), dma(1), dma(units),
-            dma(2, n), dma(2, n - 1, CHUNKS),
+            dma(1), dma(units), dma(3), dma(units, 3), dma(1), dma(box),
+            dma(1), dma(box), dma(3), dma(units, 3), dma(1), dma(units),
+            dma(2, n), dma(2, n - 1, CHUNKS), dma(13),
         ],
         compiler_params=pltpu.CompilerParams(
             collective_id=2, has_side_effects=True, vmem_limit_bytes=60 * 1024 * 1024
         ),
         name="fused_column",
-    )(x, angle, window, u, v, plane, observed, *tables, taps, plane_angle, shift)
+    )(*arrays, taps, plane_angle, shift)
 
 
 def local(n, nf, model_strip, screen_angle, facet_window, facet_shift, kernel_taps, plane_angle, u_cell, v_cell, w_plane, observed):

time: 95.2 us -> 93.8 us (0.985)
  Pallas kernels: 90 us -> 88.5 us
    pallas_call x1, Pallas kernels: 90 us -> 88.5 us  [fused(): pl.pallas_call(functools.partial(fused_kernel, n, moved), out_shape=(jax....]
where the time goes in v3:
time: 93.8 us; the launch traced here: 93.6 us
  Pallas kernels  88.5 us (94%)
  local copies, waits for them, and re-layouts  3.77 us (4%)
  between operations  1.29 us (1%)
    pallas_call x1, Pallas kernels, fused(): pl.pallas_call(functools.partial(fused_kernel, n, moved), out_shape=(jax....  88.5 us
    unnamed x2, local copies, waits for them, and re-layouts  3.77 us

profile of v3, /device:TPU:0, one launch (start us, length us, event | category | flops | bytes accessed | tf_op | source)
XLA Modules:
  0.0 93.6 jit_solution(1076705982515274934)
XLA Ops:
  1.3 88.5 %fused_column.1 = (f32[16,2,512]{2,1,0:T(2,128)}, f32[2,64,2048]{2,1,0:T(8,128)}) custom-call(bf16[2,64,2048]{2,1,0:T(8,128)(2,1)} %bitcast.11, bf16[64,8192]{1,0:T(8,128)(2,1)} %bitcast.9, f32[64,128]{1,0:T(8,128)} %bitcast.14, s32[16,512]{1,0:T(8,128)} %bitcast.15, s32[16,512]{1,0:T(8,128)} %bitcast.16, s32[16,512]{1,0:T(8,128)} %bitcast.17, ...), custom_call_target="tpu_custom_call" | custom-call | tf_op jit(solution)/shard_map/fused_column/pallas_call | solution.py:935
  89.8 1.5 %copy.21 = f32[1,16,2,512]{3,2,1,0:T(2,128)} copy(f32[1,16,2,512]{3,2,1,0:T(2,128)} %bitcast.13) | data formatting | bytes 131072
  91.3 2.3 %copy.22 = f32[1,2,64,2048]{3,2,1,0:T(8,128)} copy(f32[1,2,64,2048]{3,2,1,0:T(8,128)} %bitcast.10) | data formatting | bytes 2097152

commit v4 on v3

--- a/solution.py
+++ b/solution.py
@@ -318,12 +318,12 @@
 def fused_kernel(
     n, moved, *refs,
 ):
-    sources, (taps_ref, pang_ref, shift_ref, res_ref, out_ref), held = refs[:13], refs[13:18], refs[18:31]
+    sources, (taps_ref, pang_ref, shift_ref, res_out, grad_out), held = refs[:13], refs[13:18], refs[18:31]
     (x_ref, ang_ref, win_ref, u_ref, v_ref, plane_ref, obs_ref, f1_ref, g1_ref, tw_ref, g2_ref, f2_ref, tw2_ref) = held
     (
     buf, angb, cs, fac, tmpx, tmpa, contrib, r0, acc0, r1, outbox, inbox, fin, adj, phase, row_table, column_table,
     every, term, sbuf, rbuf, otmp,
-    fs, fr, angs, angr, s0, d0, s1, d1, xs, xr, ys, yr, sa, da, sc, dc, bs, br, load,
+    fs, fr, angs, angr, s0, d0, s1, d1, xs, xr, ys, yr, sa, da, sc, dc, bs, br, load, store, res_ref, out_ref,
     ) = refs[31:]
     loads = [pltpu.make_async_copy(a, b, load.at[k]) for k, (a, b) in enumerate(zip(sources, held))]
     for one_load in loads:
@@ -669,12 +669,13 @@
         adj[0, where, :] = jnp.concatenate([back[:pairs, :rows], back[pairs:, :rows]], axis=1)
         adj[1, where, :] = jnp.concatenate([back[:pairs, rows:], back[pairs:, rows:]], axis=1)
 
-    def four(step, carry):
-        for k in range(4):
-            one(4 * step + k)
+    def eight(step, carry):
+        for k in range(8):
+            one(8 * step + k)
         return carry
 
-    lax.fori_loop(0, per // 4, four, 0)
+    lax.fori_loop(0, per // 8, eight, 0)
+    pltpu.make_async_copy(res_ref, res_out, store.at[0]).start()
 
     def own_block(unit):
         return every.at[unit, core, chip]
@@ -858,9 +859,14 @@
                 for m in range(block):
                     out_ref[p, where, m * subgrids : (m + 1) * subgrids] = otmp[p, pl.ds(m, cq, stride=block), :]
 
+            pltpu.make_async_copy(out_ref.at[:, where], grad_out.at[:, where], store.at[1]).start()
+
         return carry
 
     lax.fori_loop(0, CHUNKS + LAG * (n - 1) + SPREAD, backward_step, 0)
+
+    pltpu.make_async_copy(res_ref, res_out, store.at[0]).wait()
+    pltpu.make_async_copy(out_ref, grad_out, store.at[1]).wait()
 
     def sent(ref, sem):
         remote(ref, ref, sem, angr.at[0], "facet", other).wait_send()
@@ -939,7 +945,7 @@
             jax.ShapeDtypeStruct(x.shape, jnp.float32),
         ),
         in_specs=[pl.BlockSpec(memory_space=pltpu.HBM)] * 13 + [smem] * 3,
-        out_specs=(vmem, vmem),
+        out_specs=(pl.BlockSpec(memory_space=pltpu.HBM),) * 2,
         scratch_shapes=[
             *[pltpu.VMEM(a.shape, a.dtype) for a in arrays],
             bf(n, cols, 2, block, subgrids), bf(cq * units, rows, subgrids), f32(cq * units, 2, rows, subgrids),
@@ -954,7 +960,8 @@
             dma(2, n - 1), dma(2, n - 1, CHUNKS), dma(1), dma(box),
             dma(1), dma(units), dma(3), dma(units, 3), dma(1), dma(box),
             dma(1), dma(box), dma(3), dma(units, 3), dma(1), dma(units),
-            dma(2, n), dma(2, n - 1, CHUNKS), dma(13),
+            dma(2, n), dma(2, n - 1, CHUNKS), dma(13), dma(2),
+            f32(per, 2, vis), f32(*x.shape),
         ],
         compiler_params=pltpu.CompilerParams(
             collective_id=2, has_side_effects=True, vmem_limit_bytes=60 * 1024 * 1024

time: 93.8 us -> 92 us (0.981)
  Pallas kernels: 88.5 us -> 86.8 us
    pallas_call x1, Pallas kernels: 88.5 us -> 86.8 us  [fused(): pl.pallas_call(functools.partial(fused_kernel, n, moved), out_shape=(jax....]
where the time goes in v4:
time: 92 us; the launch traced here: 91.8 us
  Pallas kernels  86.8 us (94%)
  local copies, waits for them, and re-layouts  3.77 us (4%)
  between operations  1.29 us (1%)
    pallas_call x1, Pallas kernels, fused(): pl.pallas_call(functools.partial(fused_kernel, n, moved), out_shape=(jax....  86.8 us
    unnamed x2, local copies, waits for them, and re-layouts  3.77 us

profile of v4, /device:TPU:0, one launch (start us, length us, event | category | flops | bytes accessed | tf_op | source)
XLA Modules:
  0.0 91.8 jit_solution(8150995464753716313)
XLA Ops:
  1.3 86.8 %fused_column.1 = (f32[16,2,512]{2,1,0:T(2,128)}, f32[2,64,2048]{2,1,0:T(8,128)}) custom-call(bf16[2,64,2048]{2,1,0:T(8,128)(2,1)} %bitcast.11, bf16[64,8192]{1,0:T(8,128)(2,1)} %bitcast.9, f32[64,128]{1,0:T(8,128)} %bitcast.14, s32[16,512]{1,0:T(8,128)} %bitcast.15, s32[16,512]{1,0:T(8,128)} %bitcast.16, s32[16,512]{1,0:T(8,128)} %bitcast.17, ...), custom_call_target="tpu_custom_call" | custom-call | tf_op jit(solution)/shard_map/fused_column/pallas_call | solution.py:941
  88.1 1.5 %copy.21 = f32[1,16,2,512]{3,2,1,0:T(2,128)} copy(f32[1,16,2,512]{3,2,1,0:T(2,128)} %bitcast.13) | data formatting | bytes 131072
  89.5 2.3 %copy.22 = f32[1,2,64,2048]{3,2,1,0:T(8,128)} copy(f32[1,2,64,2048]{3,2,1,0:T(8,128)} %bitcast.10) | data formatting | bytes 2097152

commit v5 on v4

--- a/solution.py
+++ b/solution.py
@@ -669,12 +669,12 @@
         adj[0, where, :] = jnp.concatenate([back[:pairs, :rows], back[pairs:, :rows]], axis=1)
         adj[1, where, :] = jnp.concatenate([back[:pairs, rows:], back[pairs:, rows:]], axis=1)
 
-    def eight(step, carry):
-        for k in range(8):
-            one(8 * step + k)
+    def block_of(step, carry):
+        for k in range(16):
+            one(16 * step + k)
         return carry
 
-    lax.fori_loop(0, per // 8, eight, 0)
+    lax.fori_loop(0, per // 16, block_of, 0)
     pltpu.make_async_copy(res_ref, res_out, store.at[0]).start()
 
     def own_block(unit):

time: 92 us -> 91.4 us (level)
  no operation moved by 1% of the time
where the time goes in v5:
time: 91.4 us; the launch traced here: 91.2 us
  Pallas kernels  86.1 us (94%)
  local copies, waits for them, and re-layouts  3.77 us (4%)
  between operations  1.29 us (1%)
    pallas_call x1, Pallas kernels, fused(): pl.pallas_call(functools.partial(fused_kernel, n, moved), out_shape=(jax....  86.1 us
    unnamed x2, local copies, waits for them, and re-layouts  3.77 us

profile of v5, /device:TPU:0, one launch (start us, length us, event | category | flops | bytes accessed | tf_op | source)
XLA Modules:
  0.0 91.2 jit_solution(8352955893453962729)
XLA Ops:
  1.3 86.1 %fused_column.1 = (f32[16,2,512]{2,1,0:T(2,128)}, f32[2,64,2048]{2,1,0:T(8,128)}) custom-call(bf16[2,64,2048]{2,1,0:T(8,128)(2,1)} %bitcast.11, bf16[64,8192]{1,0:T(8,128)(2,1)} %bitcast.9, f32[64,128]{1,0:T(8,128)} %bitcast.14, s32[16,512]{1,0:T(8,128)} %bitcast.15, s32[16,512]{1,0:T(8,128)} %bitcast.16, s32[16,512]{1,0:T(8,128)} %bitcast.17, ...), custom_call_target="tpu_custom_call" | custom-call | tf_op jit(solution)/shard_map/fused_column/pallas_call | solution.py:941
  87.4 1.5 %copy.21 = f32[1,16,2,512]{3,2,1,0:T(2,128)} copy(f32[1,16,2,512]{3,2,1,0:T(2,128)} %bitcast.13) | data formatting | bytes 131072
  88.9 2.3 %copy.22 = f32[1,2,64,2048]{3,2,1,0:T(8,128)} copy(f32[1,2,64,2048]{3,2,1,0:T(8,128)} %bitcast.10) | data formatting | bytes 2097152
